TPU v7x, 512 devices: a whole 4x8x8 slice. The times are simulated.
512 devices in a mesh: gx: 4 (over y_hi), gy: 16 (over z, y_lo), gz: 8 (over x, core).
Axes of the slice: x: 4, y: 8 (y_hi: 4, y_lo: 2; y = y_hi * 2 + y_lo), z: 8, core: 2. Of those that a mesh axis runs over, the one named last changes fastest.
Arguments:
- nodal_scalar_values: float32 [3, 32, 128, 16384], P(None, 'gx', 'gy', 'gz'), may hold values from -6 to 6
- geometry: float32 [6, 4, 16, 2048], P(None, 'gx', 'gy', 'gz'), may hold values from -1.2 to 4, as said below
Outputs:
- assembled: float32 [3, 32, 128, 16384], P(None, 'gx', 'gy', 'gz')
Inputs may be any that keep to these rules, and one draw needn't show every extreme that they name: `geometry`: G00, G11 and G22 are positive; each off-diagonal factor is at most 0.3 times the root of the product of its two diagonal factors in magnitude.
All inputs are finite; a program needn't handle non-finite values.
Results may differ from a plain program's by a relative error of at most 0.00007.
Values sent between devices are 32-bit elements; how exact they have to be, the bound alone decides.
A program may use at most 64 MiB of HBM per device.

v0:
```python
import functools

import jax
import jax.numpy as jnp
import numpy as np
from jax import lax
from jax.experimental import pallas as pl
from jax.experimental.pallas import tpu as pltpu
from jax.sharding import PartitionSpec as P

interior_points = [
    -0.8717401485096066,
    -0.5917001814331423,
    -0.2092992179024789,
    0.2092992179024789,
    0.5917001814331423,
    0.8717401485096066,
]
MESH = pl.DeviceIdType.MESH
STEP = 256
LANES = 128
X_FIRST = True
LAG = 4


def legendre_seven(point):
    previous = 1.0
    current = point
    for order in range(1, 7):
        following = ((2 * order + 1) * point * current - order * previous) / (order + 1)
        previous = current
        current = following
    return current


def gll_tables():
    degree = 7
    points = [-1.0] + interior_points + [1.0]
    values = [legendre_seven(point) for point in points]
    node_count = degree + 1
    weights = np.array([2.0 / (degree * (degree + 1) * value * value) for value in values])
    derivative = np.zeros((node_count, node_count))
    for row_index in range(node_count):
        for col_index in range(node_count):
            if row_index != col_index:
                derivative[row_index, col_index] = values[row_index] / (
                    values[col_index] * (points[row_index] - points[col_index])
                )
    derivative[0, 0] = -degree * (degree + 1) / 4.0
    derivative[node_count - 1, node_count - 1] = degree * (degree + 1) / 4.0
    return (derivative, weights)


def halves(table):
    table = np.asarray(table, np.float32)
    high = table.astype(jnp.bfloat16)
    low = (table - high.astype(np.float32)).astype(jnp.bfloat16)
    return high, low


def tables():
    derivative, weights = gll_tables()
    eye = np.eye(8)
    plane_weight = np.kron(weights, weights)
    forward_xy = np.concatenate([np.kron(derivative, eye), np.kron(eye, derivative)], axis=0)
    back_xy = np.concatenate([np.kron(derivative.T, eye), np.kron(eye, derivative.T)], axis=1)
    back_xy = back_xy * np.tile(plane_weight, 2)[None, :]
    forward_z = np.kron(np.eye(16), derivative.T)
    back_z = np.kron(np.eye(16), derivative)
    high, low = halves(forward_xy)
    forward_xy = np.concatenate([high, high, low, low], axis=1)
    high, low = halves(back_xy)
    back_xy = np.concatenate(
        [np.concatenate([high, high], axis=1), np.concatenate([low, low], axis=1)], axis=0
    )
    high, low = halves(forward_z)
    forward_z = np.tile(np.concatenate([high, low], axis=1), (2, 1))
    high, low = halves(back_z)
    back_z = np.tile(np.concatenate([high, low], axis=1), (2, 1))
    matrices = np.concatenate([forward_xy, back_xy, forward_z, back_z], axis=0)
    plane = np.repeat(plane_weight[:, None], LANES, axis=1)
    along = np.repeat(np.tile(weights, LANES // 8)[None, :], 8, axis=0)
    scales = np.concatenate([plane, along], axis=0).astype(np.float32)
    return matrices, scales


def seat(comp, m):
    if m in (0, 7):
        return 0, 2 * comp + (1 if m == 7 else 0)
    if comp:
        return comp, m - 1
    return (m - 1) // 2, 6 + (m - 1) % 2


def split(value):
    high = value.astype(jnp.bfloat16)
    low = (value - high.astype(jnp.float32)).astype(jnp.bfloat16)
    return high, low


def product(left, right):
    return jnp.dot(left, right, preferred_element_type=jnp.float32)


def along_lanes(high, low, table):
    pieces = []
    for start in range(0, high.shape[1], LANES):
        both = jnp.concatenate(
            [high[:, start : start + LANES], low[:, start : start + LANES]], axis=1
        )
        twice = product(both, table)
        pieces.append(twice[:, :LANES] + twice[:, LANES:])
    return jnp.concatenate(pieces, axis=1)


def kernel(
    sizes,
    chunk,
    u_hbm,
    geo_hbm,
    mat_hbm,
    scale_hbm,
    out,
    u,
    geo,
    mat,
    scale,
    metric,
    local,
    x_out,
    y_out,
    x_in,
    y_in,
    corner_out,
    corner_in,
    z_out,
    z_in,
    relay,
    in_sem,
    const_sem,
    x_send,
    x_recv,
    y_send,
    y_recv,
    c_send,
    c_recv,
    z_send,
    z_recv,
    r_send,
    r_recv,
    b_send,
    b_recv,
):
    comps, _, _, total = u.shape
    count = total // chunk
    order = [0] + ([count - 1] if count > 1 else []) + list(range(1, count - 1))
    names = ("gx", "gy", "gz")
    place = {name: lax.axis_index(name) for name in names}
    below = {name: place[name] > 0 for name in names}
    above = {name: place[name] < sizes[name] - 1 for name in names}

    const_copies = [
        pltpu.make_async_copy(mat_hbm, mat, const_sem.at[0]),
        pltpu.make_async_copy(scale_hbm, scale, const_sem.at[1]),
        pltpu.make_async_copy(geo_hbm, geo, const_sem.at[2]),
    ]
    for copy in const_copies:
        copy.start()
    in_copies = {}
    for c in order:
        span = pl.ds(c * chunk, chunk)
        in_copies[c] = pltpu.make_async_copy(
            u_hbm.at[:, :, :, span], u.at[:, :, :, span], in_sem.at[c]
        )
        in_copies[c].start()

    barrier = pltpu.get_barrier_semaphore()
    for name in names:
        for there, by in ((below[name], -1), (above[name], 1)):

            @pl.when(there)
            def _(name=name, by=by):
                pl.semaphore_signal(
                    barrier, inc=1, device_id={name: place[name] + by}, device_id_type=MESH
                )

    detour = sizes["gx"] == 4
    relayed = order[: count * 3 // 4] if detour else []
    opposite = lax.rem(place["gx"] + 2, 4)
    if detour:
        pl.semaphore_signal(barrier, inc=1, device_id={"gx": opposite}, device_id_type=MESH)

    for side in range(2):
        there = below if side == 0 else above

        @pl.when(jnp.logical_not(there["gx"]))
        def _(side=side):
            x_in[side] = jnp.zeros(x_in.shape[1:], jnp.float32)

        @pl.when(jnp.logical_not(there["gy"]))
        def _(side=side):
            y_in[side] = jnp.zeros(y_in.shape[1:], jnp.float32)
            corner_in[side] = jnp.zeros(corner_in.shape[1:], jnp.float32)

        @pl.when(jnp.logical_not(there["gz"]))
        def _(side=side):
            z_in[side] = jnp.zeros(z_in.shape[1:], jnp.float32)

    for copy in const_copies:
        copy.wait()

    rows = jnp.concatenate(
        [geo[k, 0] for k in range(6)] + [jnp.zeros((2, geo.shape[-1]), jnp.float32)], axis=0
    )
    lane = lax.broadcasted_iota(jnp.int32, (8, LANES), 1)
    for tile in range(total // LANES):
        first = tile * (LANES // 8)
        block = rows[:, first // LANES * LANES : first // LANES * LANES + LANES]
        spread = jnp.take_along_axis(block, lane // 8 + first % LANES, axis=1)
        metric[:, tile * LANES : (tile + 1) * LANES] = spread * scale[64:72, :]

    def x_copy(side, c):
        span = pl.ds(c * chunk, chunk)
        return pltpu.make_async_remote_copy(
            x_out.at[side, 0, :, span],
            x_in.at[side, 0, :, span],
            x_send.at[side, c],
            x_recv.at[side, c],
            device_id={"gx": place["gx"] + (1 if side == 0 else -1)},
            device_id_type=MESH,
        )

    def bulk_copy(side, c):
        span = pl.ds(c * chunk, chunk)
        return pltpu.make_async_remote_copy(
            x_out.at[side, 1:, :, span],
            x_in.at[side, 1:, :, span],
            b_send.at[side, c],
            b_recv.at[side, c],
            device_id={"gx": place["gx"] + (1 if side == 0 else -1)},
            device_id_type=MESH,
        )

    def middle(side):
        return place["gx"] == 1 + side

    def by_way_of(side):
        return 3 * (1 - side) if X_FIRST else 3 * side

    def hop_copy(side, c):
        span = pl.ds(c * chunk, chunk)
        return pltpu.make_async_remote_copy(
            x_out.at[side, 1:, :, span],
            relay.at[:, :, span],
            b_send.at[side, c],
            r_recv.at[c],
            device_id={"gx": by_way_of(side)},
            device_id_type=MESH,
        )

    def onward_copy(side, c):
        span = pl.ds(c * chunk, chunk)
        return pltpu.make_async_remote_copy(
            relay.at[:, :, span],
            x_in.at[side, 1:, :, span],
            r_send.at[c],
            b_recv.at[side, c],
            device_id={"gx": 2 - side},
            device_id_type=MESH,
        )

    def forward(c):
        for side in range(2):

            @pl.when(place["gx"] == by_way_of(side))
            def _(side=side):
                hop_copy(side, c).wait_recv()
                onward_copy(side, c).start()

    def send_bulk(c):
        for side in range(2):
            if c in relayed:
                straight = jnp.logical_and(target("gx", side), jnp.logical_not(middle(side)))
                when_do(straight, lambda: bulk_copy(side, c).start())
                when_do(middle(side), lambda: hop_copy(side, c).start())
            else:
                when_do(target("gx", side), lambda: bulk_copy(side, c).start())

    def y_copy(side, c):
        span = pl.ds(c * chunk, chunk)
        return pltpu.make_async_remote_copy(
            y_out.at[side, :, :, span],
            y_in.at[side, :, :, span],
            y_send.at[side, c],
            y_recv.at[side, c],
            device_id={"gy": place["gy"] + (1 if side == 0 else -1)},
            device_id_type=MESH,
        )

    def c_copy(side, c):
        span = pl.ds(c * chunk, chunk)
        return pltpu.make_async_remote_copy(
            corner_out.at[side, :, span],
            corner_in.at[side, :, span],
            c_send.at[side, c],
            c_recv.at[side, c],
            device_id={"gy": place["gy"] + (1 if side == 0 else -1)},
            device_id_type=MESH,
        )

    def z_copy(side):
        return pltpu.make_async_remote_copy(
            z_out.at[side],
            z_in.at[side],
            z_send.at[side],
            z_recv.at[side],
            device_id={"gz": place["gz"] + (1 if side == 0 else -1)},
            device_id_type=MESH,
        )

    def target(name, side):
        return above[name] if side == 0 else below[name]

    def source(name, side):
        return below[name] if side == 0 else above[name]

    def when_do(condition, act):
        @pl.when(condition)
        def _():
            act()

    def corners(c):
        lanes = slice(c * chunk, (c + 1) * chunk)
        for side in range(2):
            when_do(source("gx", side), lambda: x_copy(side, c).wait_recv())
        for side in range(2):
            for comp in range(comps):
                for x_side in range(2):
                    at_row = 2 * comp + x_side
                    tile, row = seat(comp, 7 if side == 0 else 0)
                    corner_out[side, at_row : at_row + 1, lanes] = x_in[
                        x_side, tile, row : row + 1, lanes
                    ]
            when_do(target("gy", side), lambda: c_copy(side, c).start())

    forward_xy, back_xy = mat[0:128, :], mat[128:256, :]
    forward_z, back_z = mat[256:512, :], mat[512:768, :]

    greeted = sum(side[name].astype(jnp.int32) for name in names for side in (below, above))
    greeted = greeted + (1 if detour else 0)
    waiting, cornering = list(relayed), list(order)
    for at, c in enumerate(order):
        in_copies[c].wait()
        for start in range(c * chunk, (c + 1) * chunk, STEP):
            lanes = slice(start, start + STEP)
            g00, g11, g22, g01, g02, g12 = [metric[k : k + 1, lanes] for k in range(6)]
            for comp in range(comps):
                field = u[comp, :, :, lanes].reshape(64, STEP)
                high, low = split(field)
                both = product(forward_xy, jnp.concatenate([high, low, high, low], axis=0))
                grad_x, grad_y = both[:64], both[64:]
                grad_z = along_lanes(high, low, forward_z)
                flux_x = g00 * grad_x + g01 * grad_y + g02 * grad_z
                flux_y = g01 * grad_x + g11 * grad_y + g12 * grad_z
                flux_z = g02 * grad_x + g12 * grad_y + g22 * grad_z
                x_high, x_low = split(flux_x)
                y_high, y_low = split(flux_y)
                z_high, z_low = split(flux_z)
                twice = product(back_xy, jnp.concatenate([x_high, y_high, x_low, y_low], axis=0))
                terms = twice[:64] + twice[64:]
                weight = jnp.concatenate([scale[0:64, :]] * (STEP // LANES), axis=1)
                terms = terms + weight * along_lanes(z_high, z_low, back_z)
                terms = terms.reshape(8, 8, STEP)
                local[comp, :, :, lanes] = terms
                for n in range(8):
                    y_out[0, comp, n : n + 1, lanes] = terms[n, 7:8]
                    y_out[1, comp, n : n + 1, lanes] = terms[n, 0:1]
                    tile, row = seat(comp, n)
                    x_out[0, tile, row : row + 1, lanes] = terms[7, n : n + 1]
                    x_out[1, tile, row : row + 1, lanes] = terms[0, n : n + 1]
        if at == 0:
            pl.semaphore_wait(barrier, greeted)
        for side in range(2):
            when_do(target("gx", side), lambda: x_copy(side, c).start())
            when_do(target("gy", side), lambda: y_copy(side, c).start())
        if at:
            send_bulk(order[at - 1])
        if at >= LAG and cornering:
            corners(cornering.pop(0))
        if at >= LAG + 1 and waiting:
            forward(waiting.pop(0))
    send_bulk(order[-1])
    while waiting or cornering:
        if cornering:
            corners(cornering.pop(0))
        if waiting:
            forward(waiting.pop(0))

    def xy_sum(comp, n, lanes):
        value = local[comp, n, :, lanes]
        from_below = y_in[0, comp, n : n + 1, lanes]
        from_above = y_in[1, comp, n : n + 1, lanes]
        if n in (0, 7):
            x_side = 0 if n == 0 else 1
            at_row = 2 * comp + x_side
            seats = [seat(comp, m) for m in range(8)]
            rows = [x_in[x_side, tile, row : row + 1, lanes] for tile, row in seats]
            value = value + jnp.concatenate(rows, axis=0)
            from_below = from_below + corner_in[0, at_row : at_row + 1, lanes]
            from_above = from_above + corner_in[1, at_row : at_row + 1, lanes]
        where = lax.broadcasted_iota(jnp.int32, value.shape, 0)
        value = value + jnp.where(where == 0, from_below, 0.0)
        return value + jnp.where(where == 7, from_above, 0.0)

    def arrived(c):
        for side in range(2):
            when_do(source("gx", side), lambda: bulk_copy(side, c).wait_recv())
            when_do(source("gy", side), lambda: y_copy(side, c).wait_recv())
            when_do(source("gy", side), lambda: c_copy(side, c).wait_recv())

    def finish(first, last):
        for comp in range(comps):
            for n in range(8):
                value = xy_sum(comp, n, slice(max(first - LANES, 0), min(last + LANES, total)))
                if first == 0:
                    value = jnp.concatenate([z_in[0, comp, n], value], axis=1)
                if last == total:
                    value = jnp.concatenate([value, z_in[1, comp, n]], axis=1)
                width = value.shape[1]
                before = pltpu.roll(value, 1, 1)[:, LANES:-LANES]
                after = pltpu.roll(value, width - 1, 1)[:, LANES:-LANES]
                position = lax.broadcasted_iota(jnp.int32, before.shape, 1) % 8
                extra = jnp.where(position == 7, after, jnp.where(position == 0, before, 0.0))
                out[comp, n, :, first:last] = value[:, LANES:-LANES] + extra

    edge = order[:2] if count > 1 else order
    group = min(2 * chunk, total)
    groups = list(range(total // group))
    here = set()
    z_here = False
    for at, c in enumerate(order):
        arrived(c)
        here.add(c)
        if at == len(edge) - 1:
            for side in range(2):
                lanes = slice(total - LANES, total) if side == 0 else slice(0, LANES)
                for comp in range(comps):
                    for n in range(8):
                        z_out[side, comp, n] = xy_sum(comp, n, lanes)
                when_do(target("gz", side), lambda: z_copy(side).start())
        for g in list(groups):
            first, last = g * group // chunk, (g + 1) * group // chunk
            if all(i in here for i in range(max(first - 1, 0), min(last + 1, count))):
                groups.remove(g)
                ends = g * group, (g + 1) * group
                if not z_here and (ends[0] == 0 or ends[1] == total):
                    z_here = True
                    for side in range(2):
                        when_do(source("gz", side), lambda: z_copy(side).wait_recv())
                finish(*ends)

    for c in order:
        for side in range(2):
            when_do(target("gx", side), lambda: x_copy(side, c).wait_send())
            when_do(target("gx", side), lambda: bulk_copy(side, c).wait_send())
            when_do(target("gy", side), lambda: y_copy(side, c).wait_send())
            when_do(target("gy", side), lambda: c_copy(side, c).wait_send())
    for side in range(2):
        when_do(target("gz", side), lambda: z_copy(side).wait_send())
        for c in relayed:
            when_do(place["gx"] == by_way_of(side), lambda: onward_copy(side, c).wait_send())


def local_part(sizes, nodal_scalar_values, geometry):
    comps, _, _, total = nodal_scalar_values.shape
    chunk = min(256, total)
    count = total // chunk
    matrices, scales = tables()
    f32 = jnp.float32
    dma = pltpu.SemaphoreType.DMA
    any_space = pl.BlockSpec(memory_space=pl.ANY)
    return pl.pallas_call(
        functools.partial(kernel, sizes, chunk),
        out_shape=pltpu.VMEM(nodal_scalar_values.shape, f32),
        in_specs=[any_space] * 4,
        out_specs=pl.BlockSpec(memory_space=pltpu.VMEM),
        scratch_shapes=[
            pltpu.VMEM(nodal_scalar_values.shape, f32),
            pltpu.VMEM(geometry.shape, f32),
            pltpu.VMEM(matrices.shape, jnp.bfloat16),
            pltpu.VMEM(scales.shape, f32),
            pltpu.VMEM((8, total), f32),
            pltpu.VMEM(nodal_scalar_values.shape, f32),
            pltpu.VMEM((2, comps, 8, total), f32),
            pltpu.VMEM((2, comps, 8, total), f32),
            pltpu.VMEM((2, comps, 8, total), f32),
            pltpu.VMEM((2, comps, 8, total), f32),
            pltpu.VMEM((2, 8, total), f32),
            pltpu.VMEM((2, 8, total), f32),
            pltpu.VMEM((2, comps, 8, 8, LANES), f32),
            pltpu.VMEM((2, comps, 8, 8, LANES), f32),
            pltpu.VMEM((comps - 1, 8, total), f32),
            dma((count,)),
            dma((3,)),
            dma((2, count)),
            dma((2, count)),
            dma((2, count)),
            dma((2, count)),
            dma((2, count)),
            dma((2, count)),
            dma((2,)),
            dma((2,)),
            dma((count,)),
            dma((count,)),
            dma((2, count)),
            dma((2, count)),
        ],
        compiler_params=pltpu.CompilerParams(collective_id=0, has_side_effects=True),
        name="poisson",
    )(nodal_scalar_values, geometry, jnp.asarray(matrices), jnp.asarray(scales))


def solution(mesh):
    return jax.shard_map(
        functools.partial(local_part, dict(mesh.shape)),
        mesh=mesh,
        in_specs=(P(None, "gx", "gy", "gz"), P(None, "gx", "gy", "gz")),
        out_specs=P(None, "gx", "gy", "gz"),
        check_vma=False,
    )
```

profile of v0, /device:TPU:206, one launch (start us, length us, event | category | flops | bytes accessed | tf_op | source)
XLA Modules:
  0.0 36.5 jit_solution(6675467908151433673)
XLA Ops:
  0.0 35.4 %poisson.1 = f32[3,8,8,2048]{3,2,1,0:T(8,128)S(1)} custom-call(f32[3,8,8,2048]{3,2,1,0:T(8,128)} %u_hbm.1, f32[6,1,1,256]{3,2,1,0:T(1,128)} %geo_hbm.1, bf16[768,256]{1,0:T(8,128)(2,1)} %constant.4.clone.mat_hbm, f32[72,128]{1,0:T(8,128)} %constant.5.clone.scale_hbm), custom_call_target="tpu_custom_call" | custom-call | tf_op jit(solution)/shard_map/poisson/pallas_call | solution.py:482
  35.4 1.1 %copy.6 = f32[3,8,8,2048]{3,2,1,0:T(8,128)} copy(f32[3,8,8,2048]{3,2,1,0:T(8,128)S(1)} %poisson.1) | data formatting | bytes 3145728
where the time goes:
time: 36.7 us; the launch traced here: 36.5 us
  Pallas kernels  35.4 us (96%)
  local copies, waits for them, and re-layouts  1.15 us (3%)
    pallas_call x1, Pallas kernels, local_part(): pl.pallas_call(functools.partial(kernel, sizes, chunk), out_shape=pltpu.V...  35.4 us
    unnamed x1, local copies, waits for them, and re-layouts  1.15 us

commit v1 on v0

v1 whole, which is shorter than its diff:
```python
import functools

import jax
import jax.numpy as jnp
import numpy as np
from jax import lax
from jax.experimental import pallas as pl
from jax.experimental.pallas import tpu as pltpu
from jax.sharding import PartitionSpec as P

interior_points = [
    -0.8717401485096066,
    -0.5917001814331423,
    -0.2092992179024789,
    0.2092992179024789,
    0.5917001814331423,
    0.8717401485096066,
]
MESH = pl.DeviceIdType.MESH
CHUNK = 256
WIDE = 512
LANES = 128


def legendre_seven(point):
    previous = 1.0
    current = point
    for order in range(1, 7):
        following = ((2 * order + 1) * point * current - order * previous) / (order + 1)
        previous = current
        current = following
    return current


def gll_tables():
    degree = 7
    points = [-1.0] + interior_points + [1.0]
    values = [legendre_seven(point) for point in points]
    node_count = degree + 1
    weights = np.array([2.0 / (degree * (degree + 1) * value * value) for value in values])
    derivative = np.zeros((node_count, node_count))
    for row_index in range(node_count):
        for col_index in range(node_count):
            if row_index != col_index:
                derivative[row_index, col_index] = values[row_index] / (
                    values[col_index] * (points[row_index] - points[col_index])
                )
    derivative[0, 0] = -degree * (degree + 1) / 4.0
    derivative[node_count - 1, node_count - 1] = degree * (degree + 1) / 4.0
    return (derivative, weights)


def halves(table):
    table = np.asarray(table, np.float32)
    high = table.astype(jnp.bfloat16)
    low = (table - high.astype(np.float32)).astype(jnp.bfloat16)
    return high, low


def tables():
    derivative, weights = gll_tables()
    eye = np.eye(8)
    plane_weight = np.kron(weights, weights)
    forward_xy = np.concatenate([np.kron(derivative, eye), np.kron(eye, derivative)], axis=0)
    back_xy = np.concatenate([np.kron(derivative.T, eye), np.kron(eye, derivative.T)], axis=1)
    back_xy = back_xy * np.tile(plane_weight, 2)[None, :]
    forward_z = np.kron(np.eye(16), derivative.T)
    back_z = np.kron(np.eye(16), derivative)
    high, low = halves(forward_xy)
    forward_xy = np.concatenate([high, high, low, low], axis=1)
    high, low = halves(back_xy)
    back_xy = np.concatenate(
        [np.concatenate([high, high], axis=1), np.concatenate([low, low], axis=1)], axis=0
    )
    high, low = halves(forward_z)
    forward_z = np.tile(np.concatenate([high, low], axis=1), (2, 1))
    high, low = halves(back_z)
    back_z = np.tile(np.concatenate([high, low], axis=1), (2, 1))
    matrices = np.concatenate([forward_xy, back_xy, forward_z, back_z], axis=0)
    plane = np.repeat(plane_weight[:, None], LANES, axis=1)
    along = np.repeat(np.tile(weights, LANES // 8)[None, :], 8, axis=0)
    scales = np.concatenate([plane, along], axis=0).astype(np.float32)
    return matrices, scales


def split(value):
    high = value.astype(jnp.bfloat16)
    low = (value - high.astype(jnp.float32)).astype(jnp.bfloat16)
    return high, low


def product(left, right):
    return jnp.dot(left, right, preferred_element_type=jnp.float32)


def along_lanes(high, low, table):
    pieces = []
    for start in range(0, high.shape[1], LANES):
        both = jnp.concatenate(
            [high[:, start : start + LANES], low[:, start : start + LANES]], axis=1
        )
        twice = product(both, table)
        pieces.append(twice[:, :LANES] + twice[:, LANES:])
    return jnp.concatenate(pieces, axis=1)


def kernel(
    sizes,
    u_hbm,
    geo_hbm,
    mat_hbm,
    scale_hbm,
    out,
    u,
    geo,
    mat,
    scale,
    local,
    x_in,
    mid_out,
    mid_in,
    edge_out,
    edge_in,
    z_out,
    z_in,
    in_sem,
    const_sem,
    x_send,
    x_recv,
    mid_send,
    mid_recv,
    edge_send,
    edge_recv,
    z_send,
    z_recv,
):
    comps, _, _, total = u.shape
    count = total // CHUNK
    wides = total // WIDE
    tiles = total // LANES
    per_wide = WIDE // CHUNK
    across = WIDE // LANES
    wide_order = [0] + ([wides - 1] if wides > 1 else []) + list(range(1, wides - 1))
    order = [w * per_wide + k for w in wide_order for k in range(per_wide)]
    names = ("gx", "gy", "gz")
    place = {name: lax.axis_index(name) for name in names}
    below = {name: place[name] > 0 for name in names}
    above = {name: place[name] < sizes[name] - 1 for name in names}

    const_copies = [
        pltpu.make_async_copy(geo_hbm, geo, const_sem.at[2]),
        pltpu.make_async_copy(scale_hbm, scale, const_sem.at[1]),
        pltpu.make_async_copy(mat_hbm, mat, const_sem.at[0]),
    ]
    for copy in const_copies:
        copy.start()
    in_copies = {}
    for c in order:
        span = pl.ds(c * CHUNK, CHUNK)
        in_copies[c] = pltpu.make_async_copy(
            u_hbm.at[:, :, :, span], u.at[:, :, :, span], in_sem.at[c]
        )
        in_copies[c].start()

    barrier = pltpu.get_barrier_semaphore()
    for name in names:
        for there, by in ((below[name], -1), (above[name], 1)):

            @pl.when(there)
            def _(name=name, by=by):
                pl.semaphore_signal(
                    barrier, inc=1, device_id={name: place[name] + by}, device_id_type=MESH
                )

    def target(name, side):
        return above[name] if side == 0 else below[name]

    def source(name, side):
        return below[name] if side == 0 else above[name]

    def when_do(condition, act):
        @pl.when(condition)
        def _():
            act()

    for side in range(2):

        @pl.when(jnp.logical_not(source("gx", side)))
        def _(side=side):
            x_in[side] = jnp.zeros(x_in.shape[1:], jnp.float32)

        @pl.when(jnp.logical_not(source("gy", side)))
        def _(side=side):
            mid_in[side] = jnp.zeros(mid_in.shape[1:], jnp.float32)
            edge_in[side] = jnp.zeros(edge_in.shape[1:], jnp.float32)

        @pl.when(jnp.logical_not(source("gz", side)))
        def _(side=side):
            z_in[side] = jnp.zeros(z_in.shape[1:], jnp.float32)

    def neighbour(name, side):
        return {name: place[name] + (1 if side == 0 else -1)}

    def x_copy(side, c):
        span = pl.ds(c * CHUNK, CHUNK)
        return pltpu.make_async_remote_copy(
            local.at[:, 7 if side == 0 else 0, :, span],
            x_in.at[side, :, :, span],
            x_send.at[side, c],
            x_recv.at[side, c],
            device_id=neighbour("gx", side),
            device_id_type=MESH,
        )

    def mid_copy(side, w):
        return pltpu.make_async_remote_copy(
            mid_out.at[side, w],
            mid_in.at[side, w],
            mid_send.at[side, w],
            mid_recv.at[side, w],
            device_id=neighbour("gy", side),
            device_id_type=MESH,
        )

    def edge_copy(side, w):
        return pltpu.make_async_remote_copy(
            edge_out.at[side, w],
            edge_in.at[side, w],
            edge_send.at[side, w],
            edge_recv.at[side, w],
            device_id=neighbour("gy", side),
            device_id_type=MESH,
        )

    def z_copy(side):
        return pltpu.make_async_remote_copy(
            z_out.at[side],
            z_in.at[side],
            z_send.at[side],
            z_recv.at[side],
            device_id=neighbour("gz", side),
            device_id_type=MESH,
        )

    def mid_row(comp, n, tile):
        return (comp * 6 + n - 1) * across + tile % across

    def edge_row(comp, end, tile):
        return (comp * 2 + end) * across + tile % across

    for copy in const_copies[:2]:
        copy.wait()
    rows = jnp.concatenate(
        [geo[k, 0] for k in range(6)] + [jnp.zeros((2, geo.shape[-1]), jnp.float32)], axis=0
    )
    lane = lax.broadcasted_iota(jnp.int32, (8, LANES), 1)

    def metric_of(tile):
        first = tile * (LANES // 8)
        block = rows[:, first // LANES * LANES : first // LANES * LANES + LANES]
        spread = jnp.take_along_axis(block, lane // 8 + first % LANES, axis=1)
        return spread * scale[64:72, :]

    def compute(c):
        start = c * CHUNK
        lanes = slice(start, start + CHUNK)
        metric = jnp.concatenate(
            [metric_of(start // LANES + k) for k in range(CHUNK // LANES)], axis=1
        )
        g00, g11, g22, g01, g02, g12 = [metric[k : k + 1] for k in range(6)]
        forward_xy, back_xy = mat[0:128, :], mat[128:256, :]
        forward_z, back_z = mat[256:512, :], mat[512:768, :]
        for comp in range(comps):
            field = u[comp, :, :, lanes].reshape(64, CHUNK)
            high, low = split(field)
            both = product(forward_xy, jnp.concatenate([high, low, high, low], axis=0))
            grad_x, grad_y = both[:64], both[64:]
            grad_z = along_lanes(high, low, forward_z)
            flux_x = g00 * grad_x + g01 * grad_y + g02 * grad_z
            flux_y = g01 * grad_x + g11 * grad_y + g12 * grad_z
            flux_z = g02 * grad_x + g12 * grad_y + g22 * grad_z
            x_high, x_low = split(flux_x)
            y_high, y_low = split(flux_y)
            z_high, z_low = split(flux_z)
            twice = product(back_xy, jnp.concatenate([x_high, y_high, x_low, y_low], axis=0))
            terms = twice[:64] + twice[64:]
            weight = jnp.concatenate([scale[0:64, :]] * (CHUNK // LANES), axis=1)
            terms = terms + weight * along_lanes(z_high, z_low, back_z)
            terms = terms.reshape(8, 8, CHUNK)
            local[comp, :, :, lanes] = terms
            for n in range(1, 7):
                for k in range(CHUNK // LANES):
                    tile = start // LANES + k
                    row = mid_row(comp, n, tile)
                    part = slice(k * LANES, (k + 1) * LANES)
                    mid_out[0, tile // across, row : row + 1, :] = terms[n, 7:8, part]
                    mid_out[1, tile // across, row : row + 1, :] = terms[n, 0:1, part]

    def corners(w):
        for c in range(w * per_wide, (w + 1) * per_wide):
            for side in range(2):
                when_do(source("gx", side), lambda: x_copy(side, c).wait_recv())
        for comp in range(comps):
            for end in range(2):
                for tile in range(w * across, (w + 1) * across):
                    lanes = slice(tile * LANES, (tile + 1) * LANES)
                    value = local[comp, 7 * end, :, lanes] + x_in[end, comp, :, lanes]
                    x_in[end, comp, :, lanes] = value
                    row = edge_row(comp, end, tile)
                    edge_out[0, w, row : row + 1, :] = value[7:8]
                    edge_out[1, w, row : row + 1, :] = value[0:1]
        for side in range(2):
            when_do(target("gy", side), lambda: edge_copy(side, w).start())

    def send_mid(w):
        for side in range(2):
            when_do(target("gy", side), lambda: mid_copy(side, w).start())

    def wait_mid(w):
        for side in range(2):
            when_do(source("gy", side), lambda: mid_copy(side, w).wait_recv())

    def wait_edge(w):
        for side in range(2):
            when_do(source("gy", side), lambda: edge_copy(side, w).wait_recv())

    def xy_sum(comp, n, tile):
        lanes = slice(tile * LANES, (tile + 1) * LANES)
        w = tile // across
        if n in (0, 7):
            value = x_in[n // 7, comp, :, lanes]
            row = edge_row(comp, n // 7, tile)
            sides = [edge_in[side, w, row : row + 1, :] for side in range(2)]
        else:
            value = local[comp, n, :, lanes]
            row = mid_row(comp, n, tile)
            sides = [mid_in[side, w, row : row + 1, :] for side in range(2)]
        where = lax.broadcasted_iota(jnp.int32, value.shape, 0)
        value = value + jnp.where(where == 0, sides[0], 0.0)
        return value + jnp.where(where == 7, sides[1], 0.0)

    def finish(which, first, last):
        for comp in range(comps):
            for n in which:
                parts = []
                for tile in range(first - 1, last + 1):
                    if tile < 0:
                        parts.append(z_in[0, comp, n])
                    elif tile == tiles:
                        parts.append(z_in[1, comp, n])
                    else:
                        parts.append(xy_sum(comp, n, tile))
                value = jnp.concatenate(parts, axis=1)
                width = value.shape[1]
                before = pltpu.roll(value, 1, 1)[:, LANES:-LANES]
                after = pltpu.roll(value, width - 1, 1)[:, LANES:-LANES]
                position = lax.broadcasted_iota(jnp.int32, before.shape, 1) % 8
                extra = jnp.where(position == 7, after, jnp.where(position == 0, before, 0.0))
                out[comp, n, :, first * LANES : last * LANES] = value[:, LANES:-LANES] + extra

    middle, ends = range(1, 7), (0, 7)
    z_here = []

    def wait_z():
        if not z_here:
            z_here.append(True)
            for side in range(2):
                when_do(source("gz", side), lambda: z_copy(side).wait_recv())

    finished = {middle: set(), ends: set()}
    arrived = {middle: set(), ends: set()}

    def finish_ready(which, with_z):
        have = arrived[which]

        def near(tile):
            return tile // across in have if 0 <= tile < tiles else with_z

        ready = [
            tile
            for tile in range(tiles)
            if tile not in finished[which] and all(near(tile + k) for k in (-1, 0, 1))
        ]
        while ready:
            first = last = ready.pop(0)
            while ready and ready[0] == last + 1 and last - first < across - 1:
                last = ready.pop(0)
            finished[which].update(range(first, last + 1))
            finish(which, first, last + 1)

    greeted = sum(side[name].astype(jnp.int32) for name in names for side in (below, above))
    const_copies[2].wait()
    for at, c in enumerate(order):
        in_copies[c].wait()
        compute(c)
        if at == 0:
            pl.semaphore_wait(barrier, greeted)
        for side in range(2):
            when_do(target("gx", side), lambda: x_copy(side, c).start())
        if at == 1:
            send_mid(wide_order[0])
        if at == 4:
            send_mid(wide_order[1])
        if at == 5:
            corners(wide_order[0])
    send_mid(wide_order[2])
    corners(wide_order[1])
    send_mid(wide_order[3])
    corners(wide_order[2])
    corners(wide_order[3])

    for w in wide_order[:2]:
        wait_mid(w)
        wait_edge(w)
        arrived[middle].add(w)
        arrived[ends].add(w)
    for side in range(2):
        tile = tiles - 1 if side == 0 else 0
        for comp in range(comps):
            for n in range(8):
                z_out[side, comp, n] = xy_sum(comp, n, tile)
        when_do(target("gz", side), lambda: z_copy(side).start())
    finish_ready(middle, False)
    finish_ready(ends, False)
    wait_mid(wide_order[2])
    arrived[middle].add(wide_order[2])
    finish_ready(middle, False)
    wait_edge(wide_order[2])
    arrived[ends].add(wide_order[2])
    finish_ready(ends, False)
    wait_z()
    finish_ready(middle, True)
    finish_ready(ends, True)
    wait_mid(wide_order[3])
    arrived[middle].add(wide_order[3])
    finish_ready(middle, True)
    wait_edge(wide_order[3])
    arrived[ends].add(wide_order[3])
    finish_ready(ends, True)

    for side in range(2):
        for c in order:
            when_do(target("gx", side), lambda: x_copy(side, c).wait_send())
        for w in wide_order:
            when_do(target("gy", side), lambda: mid_copy(side, w).wait_send())
            when_do(target("gy", side), lambda: edge_copy(side, w).wait_send())
        when_do(target("gz", side), lambda: z_copy(side).wait_send())


def local_part(sizes, nodal_scalar_values, geometry):
    comps, _, _, total = nodal_scalar_values.shape
    count = total // CHUNK
    wides = total // WIDE
    across = WIDE // LANES
    matrices, scales = tables()
    f32 = jnp.float32
    dma = pltpu.SemaphoreType.DMA
    any_space = pl.BlockSpec(memory_space=pl.ANY)
    return pl.pallas_call(
        functools.partial(kernel, sizes),
        out_shape=pltpu.VMEM(nodal_scalar_values.shape, f32),
        in_specs=[any_space] * 4,
        out_specs=pl.BlockSpec(memory_space=pltpu.VMEM),
        scratch_shapes=[
            pltpu.VMEM(nodal_scalar_values.shape, f32),
            pltpu.VMEM(geometry.shape, f32),
            pltpu.VMEM(matrices.shape, jnp.bfloat16),
            pltpu.VMEM(scales.shape, f32),
            pltpu.VMEM(nodal_scalar_values.shape, f32),
            pltpu.VMEM((2, comps, 8, total), f32),
            pltpu.VMEM((2, wides, comps * 6 * across, LANES), f32),
            pltpu.VMEM((2, wides, comps * 6 * across, LANES), f32),
            pltpu.VMEM((2, wides, comps * 2 * across, LANES), f32),
            pltpu.VMEM((2, wides, comps * 2 * across, LANES), f32),
            pltpu.VMEM((2, comps, 8, 8, LANES), f32),
            pltpu.VMEM((2, comps, 8, 8, LANES), f32),
            dma((count,)),
            dma((3,)),
            dma((2, count)),
            dma((2, count)),
            dma((2, wides)),
            dma((2, wides)),
            dma((2, wides)),
            dma((2, wides)),
            dma((2,)),
            dma((2,)),
        ],
        compiler_params=pltpu.CompilerParams(collective_id=0, has_side_effects=True),
        name="poisson",
    )(nodal_scalar_values, geometry, jnp.asarray(matrices), jnp.asarray(scales))


def solution(mesh):
    return jax.shard_map(
        functools.partial(local_part, dict(mesh.shape)),
        mesh=mesh,
        in_specs=(P(None, "gx", "gy", "gz"), P(None, "gx", "gy", "gz")),
        out_specs=P(None, "gx", "gy", "gz"),
        check_vma=False,
    )
```

time: 36.7 us -> 30 us (0.82)
  the two profiles are of different devices: /device:TPU:206 before, /device:TPU:235 now
where the time goes in v1:
time: 30 us; the launch traced here: 29.8 us
  Pallas kernels  28.7 us (96%)
  local copies, waits for them, and re-layouts  1.15 us (4%)
    pallas_call x1, Pallas kernels, local_part(): pl.pallas_call(functools.partial(kernel, sizes), out_shape=pltpu.VMEM(nod...  28.7 us
    unnamed x1, local copies, waits for them, and re-layouts  1.15 us

profile of v1, /device:TPU:235, one launch (start us, length us, event | category | flops | bytes accessed | tf_op | source)
XLA Modules:
  0.0 29.8 jit_solution(11751339560908124975)
XLA Ops:
  0.0 28.7 %poisson.1 = f32[3,8,8,2048]{3,2,1,0:T(8,128)S(1)} custom-call(f32[3,8,8,2048]{3,2,1,0:T(8,128)} %u_hbm.1, f32[6,1,1,256]{3,2,1,0:T(1,128)} %geo_hbm.1, bf16[768,256]{1,0:T(8,128)(2,1)} %constant.4.clone.mat_hbm, f32[72,128]{1,0:T(8,128)} %constant.5.clone.scale_hbm), custom_call_target="tpu_custom_call" | custom-call | tf_op jit(solution)/shard_map/poisson/pallas_call | solution.py:459
  28.7 1.1 %copy.6 = f32[3,8,8,2048]{3,2,1,0:T(8,128)} copy(f32[3,8,8,2048]{3,2,1,0:T(8,128)S(1)} %poisson.1) | data formatting | bytes 3145728

commit v2 on v1

v2 whole, which is shorter than its diff:
```python
import functools

import jax
import jax.numpy as jnp
import numpy as np
from jax import lax
from jax.experimental import pallas as pl
from jax.experimental.pallas import tpu as pltpu
from jax.sharding import PartitionSpec as P

interior_points = [
    -0.8717401485096066,
    -0.5917001814331423,
    -0.2092992179024789,
    0.2092992179024789,
    0.5917001814331423,
    0.8717401485096066,
]
MESH = pl.DeviceIdType.MESH
CHUNK = 256
LANES = 128
PER = CHUNK // LANES
GROUP = 4


def plan(total):
    count, tiles = total // CHUNK, total // LANES
    order = [0, count - 1] + list(range(1, count - 1))
    rest = [c * PER + k for c in order for k in range(PER)]
    return order, [rest[at : at + GROUP] for at in range(0, tiles, GROUP)]


def offsets(groups, rows):
    places, at = [], 0
    for group in groups:
        size = -(-len(group) * rows // 8) * 8
        places.append((at, size))
        at += size
    return places, at


def legendre_seven(point):
    previous = 1.0
    current = point
    for order in range(1, 7):
        following = ((2 * order + 1) * point * current - order * previous) / (order + 1)
        previous = current
        current = following
    return current


def gll_tables():
    degree = 7
    points = [-1.0] + interior_points + [1.0]
    values = [legendre_seven(point) for point in points]
    node_count = degree + 1
    weights = np.array([2.0 / (degree * (degree + 1) * value * value) for value in values])
    derivative = np.zeros((node_count, node_count))
    for row_index in range(node_count):
        for col_index in range(node_count):
            if row_index != col_index:
                derivative[row_index, col_index] = values[row_index] / (
                    values[col_index] * (points[row_index] - points[col_index])
                )
    derivative[0, 0] = -degree * (degree + 1) / 4.0
    derivative[node_count - 1, node_count - 1] = degree * (degree + 1) / 4.0
    return (derivative, weights)


def halves(table):
    table = np.asarray(table, np.float32)
    high = table.astype(jnp.bfloat16)
    low = (table - high.astype(np.float32)).astype(jnp.bfloat16)
    return high, low


def tables():
    derivative, weights = gll_tables()
    eye = np.eye(8)
    plane_weight = np.kron(weights, weights)
    forward_xy = np.concatenate([np.kron(derivative, eye), np.kron(eye, derivative)], axis=0)
    back_xy = np.concatenate([np.kron(derivative.T, eye), np.kron(eye, derivative.T)], axis=1)
    back_xy = back_xy * np.tile(plane_weight, 2)[None, :]
    forward_z = np.kron(np.eye(16), derivative.T)
    back_z = np.kron(np.eye(16), derivative)
    high, low = halves(forward_xy)
    forward_xy = np.concatenate([high, high, low, low], axis=1)
    high, low = halves(back_xy)
    back_xy = np.concatenate(
        [np.concatenate([high, high], axis=1), np.concatenate([low, low], axis=1)], axis=0
    )
    high, low = halves(forward_z)
    forward_z = np.concatenate([high, low], axis=1)
    high, low = halves(back_z)
    back_z = np.concatenate([high, low], axis=1)
    matrices = np.concatenate([forward_xy, back_xy, forward_z, back_z], axis=0)
    plane = np.repeat(plane_weight[:, None], LANES, axis=1)
    along = np.repeat(np.tile(weights, LANES // 8)[None, :], 8, axis=0)
    scales = np.concatenate([plane, along], axis=0).astype(np.float32)
    return matrices, scales


def split(value):
    high = value.astype(jnp.bfloat16)
    low = (value - high.astype(jnp.float32)).astype(jnp.bfloat16)
    return high, low


def product(left, right):
    return jnp.dot(left, right, preferred_element_type=jnp.float32)


def along_lanes(high, low, table):
    pieces = []
    for start in range(0, high.shape[1], LANES):
        both = jnp.concatenate(
            [high[:, start : start + LANES], low[:, start : start + LANES]], axis=1
        )
        twice = product(both, table)
        pieces.append(twice[:, :LANES] + twice[:, LANES:])
    return jnp.concatenate(pieces, axis=1)


def kernel(
    sizes,
    u_hbm,
    geo_hbm,
    mat_hbm,
    scale_hbm,
    out,
    u,
    geo,
    mat,
    scale,
    local,
    x_in,
    mid_out,
    mid_in,
    edge_out,
    edge_in,
    z_out,
    z_in,
    in_sem,
    const_sem,
    x_send,
    x_recv,
    mid_send,
    mid_recv,
    edge_send,
    edge_recv,
    z_send,
    z_recv,
):
    comps, _, _, total = u.shape
    tiles = total // LANES
    order, groups = plan(total)
    mid_place, _ = offsets(groups, comps * 6)
    edge_place, _ = offsets(groups, comps * 2)
    group_of = {tile: (g, k) for g, group in enumerate(groups) for k, tile in enumerate(group)}
    names = ("gx", "gy", "gz")
    place = {name: lax.axis_index(name) for name in names}
    below = {name: place[name] > 0 for name in names}
    above = {name: place[name] < sizes[name] - 1 for name in names}

    def in_copy(at, first, last):
        span = pl.ds(first * CHUNK, (last - first) * CHUNK)
        return pltpu.make_async_copy(
            u_hbm.at[:, :, :, span], u.at[:, :, :, span], in_sem.at[at]
        )

    count = total // CHUNK
    in_copies = [in_copy(0, 0, 1), in_copy(1, count - 1, count), in_copy(2, 1, count - 1)]
    const_copies = [
        pltpu.make_async_copy(geo_hbm, geo, const_sem.at[0]),
        pltpu.make_async_copy(scale_hbm, scale, const_sem.at[1]),
        pltpu.make_async_copy(mat_hbm, mat, const_sem.at[2]),
    ]
    in_copies[0].start()
    for copy in const_copies:
        copy.start()

    barrier = pltpu.get_barrier_semaphore()
    for name in names:
        for there, by in ((below[name], -1), (above[name], 1)):

            @pl.when(there)
            def _(name=name, by=by):
                pl.semaphore_signal(
                    barrier, inc=1, device_id={name: place[name] + by}, device_id_type=MESH
                )

    for copy in in_copies[1:]:
        copy.start()

    def target(name, side):
        return above[name] if side == 0 else below[name]

    def source(name, side):
        return below[name] if side == 0 else above[name]

    def when_do(condition, act):
        @pl.when(condition)
        def _():
            act()

    for side in range(2):

        @pl.when(jnp.logical_not(source("gx", side)))
        def _(side=side):
            x_in[side] = jnp.zeros(x_in.shape[1:], jnp.float32)

        @pl.when(jnp.logical_not(source("gy", side)))
        def _(side=side):
            mid_in[side] = jnp.zeros(mid_in.shape[1:], jnp.float32)
            edge_in[side] = jnp.zeros(edge_in.shape[1:], jnp.float32)

        @pl.when(jnp.logical_not(source("gz", side)))
        def _(side=side):
            z_in[side] = jnp.zeros(z_in.shape[1:], jnp.float32)

    def neighbour(name, side):
        return {name: place[name] + (1 if side == 0 else -1)}

    def x_copy(side, first, size):
        span = pl.ds(first, size)
        return pltpu.make_async_remote_copy(
            local.at[:, 7 if side == 0 else 0, :, span],
            x_in.at[side, :, :, span],
            x_send,
            x_recv.at[first // CHUNK],
            device_id=neighbour("gx", side),
            device_id_type=MESH,
        )

    def mid_copy(side, g):
        span = pl.ds(*mid_place[g])
        return pltpu.make_async_remote_copy(
            mid_out.at[side, span],
            mid_in.at[side, span],
            mid_send,
            mid_recv.at[g],
            device_id=neighbour("gy", side),
            device_id_type=MESH,
        )

    def edge_copy(side, g):
        span = pl.ds(*edge_place[g])
        return pltpu.make_async_remote_copy(
            edge_out.at[side, span],
            edge_in.at[side, span],
            edge_send,
            edge_recv.at[g],
            device_id=neighbour("gy", side),
            device_id_type=MESH,
        )

    def z_copy(side):
        return pltpu.make_async_remote_copy(
            z_out.at[side],
            z_in.at[side],
            z_send,
            z_recv,
            device_id=neighbour("gz", side),
            device_id_type=MESH,
        )

    def take_both(name, ref, part, semaphore):
        both = jnp.logical_and(below[name], above[name])
        one = jnp.logical_xor(below[name], above[name])
        for condition, sides in ((both, 2), (one, 1)):
            piece = ref.at[(pl.ds(0, sides),) + part]
            when_do(condition, lambda: pltpu.make_async_copy(piece, piece, semaphore).wait())

    def mid_row(comp, n, tile):
        g, k = group_of[tile]
        return mid_place[g][0] + k * comps * 6 + comp * 6 + n - 1

    def edge_row(comp, end, tile):
        g, k = group_of[tile]
        return edge_place[g][0] + k * comps * 2 + comp * 2 + end

    for copy in const_copies[:2]:
        copy.wait()
    rows = jnp.concatenate(
        [geo[k, 0] for k in range(6)] + [jnp.zeros((2, geo.shape[-1]), jnp.float32)], axis=0
    )
    lane = lax.broadcasted_iota(jnp.int32, (8, LANES), 1)

    def metric_of(tile):
        first = tile * (LANES // 8)
        block = rows[:, first // LANES * LANES : first // LANES * LANES + LANES]
        spread = jnp.take_along_axis(block, lane // 8 + first % LANES, axis=1)
        return spread * scale[64:72, :]

    def compute(start, size):
        lanes = slice(start, start + size)
        metric = jnp.concatenate(
            [metric_of(start // LANES + k) for k in range(size // LANES)], axis=1
        )
        g00, g11, g22, g01, g02, g12 = [metric[k : k + 1] for k in range(6)]
        forward_xy, back_xy = mat[0:128, :], mat[128:256, :]
        forward_z = jnp.concatenate([mat[256:384, :]] * 2, axis=0)
        back_z = jnp.concatenate([mat[384:512, :]] * 2, axis=0)
        for comp in range(comps):
            field = u[comp, :, :, lanes].reshape(64, size)
            high, low = split(field)
            both = product(forward_xy, jnp.concatenate([high, low, high, low], axis=0))
            grad_x, grad_y = both[:64], both[64:]
            grad_z = along_lanes(high, low, forward_z)
            flux_x = g00 * grad_x + g01 * grad_y + g02 * grad_z
            flux_y = g01 * grad_x + g11 * grad_y + g12 * grad_z
            flux_z = g02 * grad_x + g12 * grad_y + g22 * grad_z
            x_high, x_low = split(flux_x)
            y_high, y_low = split(flux_y)
            z_high, z_low = split(flux_z)
            twice = product(back_xy, jnp.concatenate([x_high, y_high, x_low, y_low], axis=0))
            terms = twice[:64] + twice[64:]
            weight = jnp.concatenate([scale[0:64, :]] * (size // LANES), axis=1)
            terms = terms + weight * along_lanes(z_high, z_low, back_z)
            terms = terms.reshape(8, 8, size)
            local[comp, :, :, lanes] = terms
            for n in range(1, 7):
                for k in range(size // LANES):
                    row = mid_row(comp, n, start // LANES + k)
                    part = slice(k * LANES, (k + 1) * LANES)
                    mid_out[0, row : row + 1, :] = terms[n, 7:8, part]
                    mid_out[1, row : row + 1, :] = terms[n, 0:1, part]

    x_here = set()

    def wait_x(c):
        if c not in x_here:
            x_here.add(c)
            span = pl.ds(c * CHUNK, CHUNK)
            take_both("gx", x_in, (slice(None), slice(None), span), x_recv.at[c])

    def corners(g):
        for tile in groups[g]:
            wait_x(tile // PER)
        for comp in range(comps):
            for end in range(2):
                for tile in groups[g]:
                    lanes = slice(tile * LANES, (tile + 1) * LANES)
                    value = local[comp, 7 * end, :, lanes] + x_in[end, comp, :, lanes]
                    x_in[end, comp, :, lanes] = value
                    row = edge_row(comp, end, tile)
                    edge_out[0, row : row + 1, :] = value[7:8]
                    edge_out[1, row : row + 1, :] = value[0:1]
        for side in range(2):
            when_do(target("gy", side), lambda: edge_copy(side, g).start())

    def send_mid(g):
        for side in range(2):
            when_do(target("gy", side), lambda: mid_copy(side, g).start())

    def wait_mid(g):
        take_both("gy", mid_in, (pl.ds(*mid_place[g]),), mid_recv.at[g])

    def wait_edge(g):
        take_both("gy", edge_in, (pl.ds(*edge_place[g]),), edge_recv.at[g])

    def xy_sum(comp, n, tile):
        lanes = slice(tile * LANES, (tile + 1) * LANES)
        if n in (0, 7):
            value = x_in[n // 7, comp, :, lanes]
            row = edge_row(comp, n // 7, tile)
            sides = [edge_in[side, row : row + 1, :] for side in range(2)]
        else:
            value = local[comp, n, :, lanes]
            row = mid_row(comp, n, tile)
            sides = [mid_in[side, row : row + 1, :] for side in range(2)]
        where = lax.broadcasted_iota(jnp.int32, value.shape, 0)
        value = value + jnp.where(where == 0, sides[0], 0.0)
        return value + jnp.where(where == 7, sides[1], 0.0)

    def send_z():
        for side in range(2):
            tile, column = (tiles - 1, LANES - 1) if side == 0 else (0, 0)
            packed = jnp.zeros((8, LANES), jnp.float32)
            for comp in range(comps):
                for n in range(8):
                    value = xy_sum(comp, n, tile)[:, column : column + 1]
                    packed = jnp.where(lane == comp * 8 + n, value, packed)
            z_out[side] = packed
            when_do(target("gz", side), lambda: z_copy(side).start())

    def z_column(side, comp, n):
        at = comp * 8 + n
        return jnp.broadcast_to(z_in[side, :, at : at + 1], (8, LANES))

    def finish(which, first, last):
        for comp in range(comps):
            for n in which:
                parts = []
                for tile in range(first - 1, last + 1):
                    if tile < 0:
                        parts.append(z_column(0, comp, n))
                    elif tile == tiles:
                        parts.append(z_column(1, comp, n))
                    else:
                        parts.append(xy_sum(comp, n, tile))
                value = jnp.concatenate(parts, axis=1)
                width = value.shape[1]
                before = pltpu.roll(value, 1, 1)[:, LANES:-LANES]
                after = pltpu.roll(value, width - 1, 1)[:, LANES:-LANES]
                position = lax.broadcasted_iota(jnp.int32, before.shape, 1) % 8
                extra = jnp.where(position == 7, after, jnp.where(position == 0, before, 0.0))
                out[comp, n, :, first * LANES : last * LANES] = value[:, LANES:-LANES] + extra

    middle, ends = range(1, 7), (0, 7)
    def wait_z():
        take_both("gz", z_in, (), z_recv)

    finished = {middle: set(), ends: set()}
    arrived = {middle: set(), ends: set()}

    def finish_ready(which, with_z):
        have = arrived[which]

        def near(tile):
            return tile in have if 0 <= tile < tiles else with_z

        ready = [
            tile
            for tile in range(tiles)
            if tile not in finished[which] and all(near(tile + k) for k in (-1, 0, 1))
        ]
        while ready:
            first = last = ready.pop(0)
            while ready and ready[0] == last + 1 and last - first < GROUP - 1:
                last = ready.pop(0)
            finished[which].update(range(first, last + 1))
            finish(which, first, last + 1)

    greeted = sum(side[name].astype(jnp.int32) for name in names for side in (below, above))
    const_copies[2].wait()
    for at, c in enumerate(order):
        if at < 3:
            in_copies[at].wait()
        steps = [(c * CHUNK, CHUNK)]
        if at == 0:
            steps = [(c * CHUNK + k * LANES, LANES) for k in range(PER)]
        for start, size in steps:
            compute(start, size)
            if start == 0:
                pl.semaphore_wait(barrier, greeted)
            for side in range(2):
                when_do(target("gx", side), lambda: x_copy(side, start, size).start())
        if at == 1:
            send_mid(0)
        if at == 5:
            corners(0)
        if at == 6:
            send_mid(1)
    send_mid(2)
    send_mid(3)

    def take(which, g, wait, with_z):
        wait(g)
        arrived[which].update(groups[g])
        finish_ready(which, with_z)

    corners(1)
    wait_mid(0)
    wait_edge(0)
    send_z()
    arrived[middle].update(groups[0])
    arrived[ends].update(groups[0])
    corners(2)
    corners(3)
    take(middle, 1, wait_mid, False)
    take(middle, 2, wait_mid, False)
    wait_z()
    take(middle, 3, wait_mid, True)
    for g in range(1, 4):
        take(ends, g, wait_edge, True)

    for name, ref, semaphore in (
        ("gx", x_in, x_send),
        ("gy", mid_in, mid_send),
        ("gy", edge_in, edge_send),
        ("gz", z_in, z_send),
    ):
        take_both(name, ref, (), semaphore)


def local_part(sizes, nodal_scalar_values, geometry):
    comps, _, _, total = nodal_scalar_values.shape
    count = total // CHUNK
    _, groups = plan(total)
    mid_rows = offsets(groups, comps * 6)[1]
    edge_rows = offsets(groups, comps * 2)[1]
    matrices, scales = tables()
    f32 = jnp.float32
    dma = pltpu.SemaphoreType.DMA
    any_space = pl.BlockSpec(memory_space=pl.ANY)
    return pl.pallas_call(
        functools.partial(kernel, sizes),
        out_shape=pltpu.VMEM(nodal_scalar_values.shape, f32),
        in_specs=[any_space] * 4,
        out_specs=pl.BlockSpec(memory_space=pltpu.VMEM),
        scratch_shapes=[
            pltpu.VMEM(nodal_scalar_values.shape, f32),
            pltpu.VMEM(geometry.shape, f32),
            pltpu.VMEM(matrices.shape, jnp.bfloat16),
            pltpu.VMEM(scales.shape, f32),
            pltpu.VMEM(nodal_scalar_values.shape, f32),
            pltpu.VMEM((2, comps, 8, total), f32),
            pltpu.VMEM((2, mid_rows, LANES), f32),
            pltpu.VMEM((2, mid_rows, LANES), f32),
            pltpu.VMEM((2, edge_rows, LANES), f32),
            pltpu.VMEM((2, edge_rows, LANES), f32),
            pltpu.VMEM((2, 8, LANES), f32),
            pltpu.VMEM((2, 8, LANES), f32),
            dma((3,)),
            dma((3,)),
            dma,
            dma((count,)),
            dma,
            dma((len(groups),)),
            dma,
            dma((len(groups),)),
            dma,
            dma,
        ],
        compiler_params=pltpu.CompilerParams(collective_id=0, has_side_effects=True),
        name="poisson",
    )(nodal_scalar_values, geometry, jnp.asarray(matrices), jnp.asarray(scales))


def solution(mesh):
    return jax.shard_map(
        functools.partial(local_part, dict(mesh.shape)),
        mesh=mesh,
        in_specs=(P(None, "gx", "gy", "gz"), P(None, "gx", "gy", "gz")),
        out_specs=P(None, "gx", "gy", "gz"),
        check_vma=False,
    )
```

time: 30 us -> 27.2 us (0.907)
  the two profiles are of different devices: /device:TPU:235 before, /device:TPU:216 now
where the time goes in v2:
time: 27.2 us; the launch traced here: 27.1 us
  Pallas kernels  25.9 us (95%)
  local copies, waits for them, and re-layouts  1.15 us (4%)
    pallas_call x1, Pallas kernels, local_part(): pl.pallas_call(functools.partial(kernel, sizes), out_shape=pltpu.VMEM(nod...  25.9 us
    unnamed x1, local copies, waits for them, and re-layouts  1.15 us

profile of v2, /device:TPU:216, one launch (start us, length us, event | category | flops | bytes accessed | tf_op | source)
XLA Modules:
  0.0 27.1 jit_solution(1299044439344859513)
XLA Ops:
  0.0 25.9 %poisson.1 = f32[3,8,8,2048]{3,2,1,0:T(8,128)S(1)} custom-call(f32[3,8,8,2048]{3,2,1,0:T(8,128)} %u_hbm.1, f32[6,1,1,256]{3,2,1,0:T(1,128)} %geo_hbm.1, bf16[512,256]{1,0:T(8,128)(2,1)} %constant.4.clone.mat_hbm, f32[72,128]{1,0:T(8,128)} %constant.5.clone.scale_hbm), custom_call_target="tpu_custom_call" | custom-call | tf_op jit(solution)/shard_map/poisson/pallas_call | solution.py:497
  25.9 1.1 %copy.6 = f32[3,8,8,2048]{3,2,1,0:T(8,128)} copy(f32[3,8,8,2048]{3,2,1,0:T(8,128)S(1)} %poisson.1) | data formatting | bytes 3145728

commit v3 on v2

--- a/solution.py
+++ b/solution.py
@@ -162,6 +162,16 @@
     below = {name: place[name] > 0 for name in names}
     above = {name: place[name] < sizes[name] - 1 for name in names}
 
+    barrier = pltpu.get_barrier_semaphore()
+    for name in names:
+        for there, by in ((below[name], -1), (above[name], 1)):
+
+            @pl.when(there)
+            def _(name=name, by=by):
+                pl.semaphore_signal(
+                    barrier, inc=1, device_id={name: place[name] + by}, device_id_type=MESH
+                )
+
     def in_copy(at, first, last):
         span = pl.ds(first * CHUNK, (last - first) * CHUNK)
         return pltpu.make_async_copy(
@@ -179,16 +189,6 @@
     for copy in const_copies:
         copy.start()
 
-    barrier = pltpu.get_barrier_semaphore()
-    for name in names:
-        for there, by in ((below[name], -1), (above[name], 1)):
-
-            @pl.when(there)
-            def _(name=name, by=by):
-                pl.semaphore_signal(
-                    barrier, inc=1, device_id={name: place[name] + by}, device_id_type=MESH
-                )
-
     for copy in in_copies[1:]:
         copy.start()
 
@@ -221,13 +221,13 @@
     def neighbour(name, side):
         return {name: place[name] + (1 if side == 0 else -1)}
 
-    def x_copy(side, first, size):
-        span = pl.ds(first, size)
+    def x_copy(side, c):
+        span = pl.ds(c * CHUNK, CHUNK)
         return pltpu.make_async_remote_copy(
             local.at[:, 7 if side == 0 else 0, :, span],
             x_in.at[side, :, :, span],
             x_send,
-            x_recv.at[first // CHUNK],
+            x_recv.at[c],
             device_id=neighbour("gx", side),
             device_id_type=MESH,
         )
@@ -437,15 +437,11 @@
     for at, c in enumerate(order):
         if at < 3:
             in_copies[at].wait()
-        steps = [(c * CHUNK, CHUNK)]
+        compute(c * CHUNK, CHUNK)
         if at == 0:
-            steps = [(c * CHUNK + k * LANES, LANES) for k in range(PER)]
-        for start, size in steps:
-            compute(start, size)
-            if start == 0:
-                pl.semaphore_wait(barrier, greeted)
-            for side in range(2):
-                when_do(target("gx", side), lambda: x_copy(side, start, size).start())
+            pl.semaphore_wait(barrier, greeted)
+        for side in range(2):
+            when_do(target("gx", side), lambda: x_copy(side, c).start())
         if at == 1:
             send_mid(0)
         if at == 5:

time: 27.2 us -> 26.8 us (0.985)
  the two profiles are of different devices: /device:TPU:216 before, /device:TPU:238 now
where the time goes in v3:
time: 26.8 us; the launch traced here: 26.7 us
  Pallas kernels  25.5 us (95%)
  local copies, waits for them, and re-layouts  1.15 us (4%)
    pallas_call x1, Pallas kernels, local_part(): pl.pallas_call(functools.partial(kernel, sizes), out_shape=pltpu.VMEM(nod...  25.5 us
    unnamed x1, local copies, waits for them, and re-layouts  1.15 us

profile of v3, /device:TPU:238, one launch (start us, length us, event | category | flops | bytes accessed | tf_op | source)
XLA Modules:
  0.0 26.7 jit_solution(10445088415885554138)
XLA Ops:
  0.0 25.5 %poisson.1 = f32[3,8,8,2048]{3,2,1,0:T(8,128)S(1)} custom-call(f32[3,8,8,2048]{3,2,1,0:T(8,128)} %u_hbm.1, f32[6,1,1,256]{3,2,1,0:T(1,128)} %geo_hbm.1, bf16[512,256]{1,0:T(8,128)(2,1)} %constant.4.clone.mat_hbm, f32[72,128]{1,0:T(8,128)} %constant.5.clone.scale_hbm), custom_call_target="tpu_custom_call" | custom-call | tf_op jit(solution)/shard_map/poisson/pallas_call | solution.py:493
  25.5 1.1 %copy.6 = f32[3,8,8,2048]{3,2,1,0:T(8,128)} copy(f32[3,8,8,2048]{3,2,1,0:T(8,128)S(1)} %poisson.1) | data formatting | bytes 3145728

commit v4 on v3

--- a/solution.py
+++ b/solution.py
@@ -21,12 +21,14 @@
 LANES = 128
 PER = CHUNK // LANES
 GROUP = 4
+LINES = 8
 
 
 def plan(total):
     count, tiles = total // CHUNK, total // LANES
-    order = [0, count - 1] + list(range(1, count - 1))
-    rest = [c * PER + k for c in order for k in range(PER)]
+    order = [1, 2, 0, count - 1] + list(range(3, count - 1))
+    late = list(range(1, count - 1)) + [0, count - 1]
+    rest = [c * PER + k for c in late for k in range(PER)]
     return order, [rest[at : at + GROUP] for at in range(0, tiles, GROUP)]
 
 
@@ -136,8 +138,12 @@
     x_in,
     mid_out,
     mid_in,
-    edge_out,
-    edge_in,
+    leaf_out,
+    hub_own,
+    hub_in,
+    hub_out,
+    hub_x,
+    line_sum,
     z_out,
     z_in,
     in_sem,
@@ -146,8 +152,12 @@
     x_recv,
     mid_send,
     mid_recv,
-    edge_send,
-    edge_recv,
+    leaf_send,
+    leaf_recv,
+    hub_send,
+    hub_recv,
+    sum_send,
+    sum_recv,
     z_send,
     z_recv,
 ):
@@ -155,13 +165,35 @@
     tiles = total // LANES
     order, groups = plan(total)
     mid_place, _ = offsets(groups, comps * 6)
-    edge_place, _ = offsets(groups, comps * 2)
+    line_tiles = [tile for group in groups for tile in group]
+    line_at = {tile: k for k, tile in enumerate(line_tiles)}
+    line_rows = LINES * comps
     group_of = {tile: (g, k) for g, group in enumerate(groups) for k, tile in enumerate(group)}
     names = ("gx", "gy", "gz")
     place = {name: lax.axis_index(name) for name in names}
     below = {name: place[name] > 0 for name in names}
     above = {name: place[name] < sizes[name] - 1 for name in names}
 
+    def target(name, side):
+        return above[name] if side == 0 else below[name]
+
+    def source(name, side):
+        return below[name] if side == 0 else above[name]
+
+    def when_do(condition, act):
+        @pl.when(condition)
+        def _():
+            act()
+
+    upper = lax.rem(place["gy"], 2)
+    lower = 1 - upper
+    inside = jnp.logical_and(below["gy"], above["gy"])
+    facing = place["gx"] + upper - lower
+    paired = jnp.logical_and(facing >= 0, facing < sizes["gx"])
+
+    def across(side):
+        return {"gx": facing, "gy": place["gy"] + (1 if side else -1)}
+
     barrier = pltpu.get_barrier_semaphore()
     for name in names:
         for there, by in ((below[name], -1), (above[name], 1)):
@@ -172,6 +204,15 @@
                     barrier, inc=1, device_id={name: place[name] + by}, device_id_type=MESH
                 )
 
+    greeted = sum(side[name].astype(jnp.int32) for name in names for side in (below, above))
+    for side in range(2):
+        there = jnp.logical_and(paired, source("gy", side))
+        greeted = greeted + there.astype(jnp.int32)
+
+        @pl.when(there)
+        def _(side=side):
+            pl.semaphore_signal(barrier, inc=1, device_id=across(side), device_id_type=MESH)
+
     def in_copy(at, first, last):
         span = pl.ds(first * CHUNK, (last - first) * CHUNK)
         return pltpu.make_async_copy(
@@ -179,7 +220,12 @@
         )
 
     count = total // CHUNK
-    in_copies = [in_copy(0, 0, 1), in_copy(1, count - 1, count), in_copy(2, 1, count - 1)]
+    in_copies = [
+        in_copy(0, 1, 2),
+        in_copy(1, 2, count - 1),
+        in_copy(2, 0, 1),
+        in_copy(3, count - 1, count),
+    ]
     const_copies = [
         pltpu.make_async_copy(geo_hbm, geo, const_sem.at[0]),
         pltpu.make_async_copy(scale_hbm, scale, const_sem.at[1]),
@@ -192,17 +238,6 @@
     for copy in in_copies[1:]:
         copy.start()
 
-    def target(name, side):
-        return above[name] if side == 0 else below[name]
-
-    def source(name, side):
-        return below[name] if side == 0 else above[name]
-
-    def when_do(condition, act):
-        @pl.when(condition)
-        def _():
-            act()
-
     for side in range(2):
 
         @pl.when(jnp.logical_not(source("gx", side)))
@@ -212,20 +247,23 @@
         @pl.when(jnp.logical_not(source("gy", side)))
         def _(side=side):
             mid_in[side] = jnp.zeros(mid_in.shape[1:], jnp.float32)
-            edge_in[side] = jnp.zeros(edge_in.shape[1:], jnp.float32)
 
         @pl.when(jnp.logical_not(source("gz", side)))
         def _(side=side):
             z_in[side] = jnp.zeros(z_in.shape[1:], jnp.float32)
 
+    @pl.when(jnp.logical_not(paired))
+    def _():
+        hub_x[...] = jnp.zeros(hub_x.shape, jnp.float32)
+
     def neighbour(name, side):
         return {name: place[name] + (1 if side == 0 else -1)}
 
-    def x_copy(side, c):
+    def x_copy(side, c, rows):
         span = pl.ds(c * CHUNK, CHUNK)
         return pltpu.make_async_remote_copy(
-            local.at[:, 7 if side == 0 else 0, :, span],
-            x_in.at[side, :, :, span],
+            local.at[:, 7 if side == 0 else 0, rows, span],
+            x_in.at[side, :, rows, span],
             x_send,
             x_recv.at[c],
             device_id=neighbour("gx", side),
@@ -243,14 +281,36 @@
             device_id_type=MESH,
         )
 
-    def edge_copy(side, g):
-        span = pl.ds(*edge_place[g])
+    def line_span(h):
+        return pl.ds(h * line_rows, line_rows)
+
+    def leaf_copy(side, h):
         return pltpu.make_async_remote_copy(
-            edge_out.at[side, span],
-            edge_in.at[side, span],
-            edge_send,
-            edge_recv.at[g],
+            leaf_out.at[side, line_span(h)],
+            hub_in.at[side, line_span(h)],
+            leaf_send,
+            leaf_recv.at[h],
             device_id=neighbour("gy", side),
+            device_id_type=MESH,
+        )
+
+    def hub_copy(side, h):
+        return pltpu.make_async_remote_copy(
+            hub_out.at[side, line_span(h)],
+            hub_x.at[1 - side, line_span(h)],
+            hub_send,
+            hub_recv.at[h],
+            device_id=across(side),
+            device_id_type=MESH,
+        )
+
+    def sum_copy(side, h):
+        return pltpu.make_async_remote_copy(
+            line_sum.at[upper, side, line_span(h)],
+            line_sum.at[upper, 1 - side, line_span(h)],
+            sum_send,
+            sum_recv.at[h],
+            device_id={"gy": place["gy"] + (1 if side else -1)},
             device_id_type=MESH,
         )
 
@@ -264,20 +324,40 @@
             device_id_type=MESH,
         )
 
-    def take_both(name, ref, part, semaphore):
+    every = slice(None)
+    within = pl.ds(1, 6)
+
+    def take_both(name, piece, semaphore, also=None):
         both = jnp.logical_and(below[name], above[name])
         one = jnp.logical_xor(below[name], above[name])
         for condition, sides in ((both, 2), (one, 1)):
-            piece = ref.at[(pl.ds(0, sides),) + part]
-            when_do(condition, lambda: pltpu.make_async_copy(piece, piece, semaphore).wait())
+            ref = piece(pl.ds(0, sides))
+            if also is not None:
+                condition = jnp.logical_and(condition, also)
+            when_do(condition, lambda: pltpu.make_async_copy(ref, ref, semaphore).wait())
+
+    def take_x(span, semaphore):
+        for rows, also in ((within, inside), (every, jnp.logical_not(inside))):
+            take_both("gx", lambda sides: x_in.at[sides, :, rows, span], semaphore, also)
+
+    def way(side, near):
+        near_side = (upper if side else lower) > 0
+        return near_side if near else jnp.logical_not(near_side)
+
+    def send_x(c, near=None):
+        for side in range(2):
+            there = target("gx", side)
+            if near is not None:
+                there = jnp.logical_and(there, way(side, near))
+            for rows, also in ((within, inside), (every, jnp.logical_not(inside))):
+                when_do(jnp.logical_and(there, also), lambda: x_copy(side, c, rows).start())
 
     def mid_row(comp, n, tile):
         g, k = group_of[tile]
         return mid_place[g][0] + k * comps * 6 + comp * 6 + n - 1
 
-    def edge_row(comp, end, tile):
-        g, k = group_of[tile]
-        return edge_place[g][0] + k * comps * 2 + comp * 2 + end
+    def line_row(comp, tile):
+        return line_at[tile] * comps + comp
 
     for copy in const_copies[:2]:
         copy.wait()
@@ -301,104 +381,162 @@
         forward_xy, back_xy = mat[0:128, :], mat[128:256, :]
         forward_z = jnp.concatenate([mat[256:384, :]] * 2, axis=0)
         back_z = jnp.concatenate([mat[384:512, :]] * 2, axis=0)
+        pieces = range(0, size, LANES)
+
+        def along_all(pairs, table):
+            blocks = [
+                jnp.concatenate([part[:, at : at + LANES] for part in pair], axis=1)
+                for pair in pairs
+                for at in pieces
+            ]
+            twice = product(jnp.concatenate(blocks, axis=0), table)
+            sums = twice[:, :LANES] + twice[:, LANES:]
+            sums = [sums[64 * k : 64 * (k + 1)] for k in range(len(blocks))]
+            count = len(pieces)
+            return [
+                jnp.concatenate(sums[k * count : (k + 1) * count], axis=1)
+                for k in range(len(pairs))
+            ]
+
+        fields = [split(u[comp, :, :, lanes].reshape(64, size)) for comp in range(comps)]
+        grads_z = along_all(fields, forward_z)
+        partial, fluxes_z = [], []
         for comp in range(comps):
-            field = u[comp, :, :, lanes].reshape(64, size)
-            high, low = split(field)
+            high, low = fields[comp]
             both = product(forward_xy, jnp.concatenate([high, low, high, low], axis=0))
-            grad_x, grad_y = both[:64], both[64:]
-            grad_z = along_lanes(high, low, forward_z)
+            grad_x, grad_y, grad_z = both[:64], both[64:], grads_z[comp]
             flux_x = g00 * grad_x + g01 * grad_y + g02 * grad_z
             flux_y = g01 * grad_x + g11 * grad_y + g12 * grad_z
             flux_z = g02 * grad_x + g12 * grad_y + g22 * grad_z
             x_high, x_low = split(flux_x)
             y_high, y_low = split(flux_y)
-            z_high, z_low = split(flux_z)
+            fluxes_z.append(split(flux_z))
             twice = product(back_xy, jnp.concatenate([x_high, y_high, x_low, y_low], axis=0))
-            terms = twice[:64] + twice[64:]
-            weight = jnp.concatenate([scale[0:64, :]] * (size // LANES), axis=1)
-            terms = terms + weight * along_lanes(z_high, z_low, back_z)
+            partial.append(twice[:64] + twice[64:])
+        weight = jnp.concatenate([scale[0:64, :]] * (size // LANES), axis=1)
+        terms_z = along_all(fluxes_z, back_z)
+        for comp in range(comps):
+            terms = partial[comp] + weight * terms_z[comp]
             terms = terms.reshape(8, 8, size)
             local[comp, :, :, lanes] = terms
-            for n in range(1, 7):
-                for k in range(size // LANES):
-                    row = mid_row(comp, n, start // LANES + k)
-                    part = slice(k * LANES, (k + 1) * LANES)
-                    mid_out[0, row : row + 1, :] = terms[n, 7:8, part]
-                    mid_out[1, row : row + 1, :] = terms[n, 0:1, part]
+            for k in range(size // LANES):
+                tile = start // LANES + k
+                if tile in (0, tiles - 1):
+                    continue
+                part = slice(k * LANES, (k + 1) * LANES)
+                for n in range(1, 7):
+                    put_mid(comp, n, tile, terms[n, :, part])
+
+    def put_mid(comp, n, tile, value):
+        row = mid_row(comp, n, tile)
+        mid_out[0, row : row + 1, :] = value[7:8]
+        mid_out[1, row : row + 1, :] = value[0:1]
 
     x_here = set()
 
-    def wait_x(c):
+    def wait_x(tile):
+        c = tile // PER
         if c not in x_here:
             x_here.add(c)
-            span = pl.ds(c * CHUNK, CHUNK)
-            take_both("gx", x_in, (slice(None), slice(None), span), x_recv.at[c])
-
-    def corners(g):
-        for tile in groups[g]:
-            wait_x(tile // PER)
-        for comp in range(comps):
-            for end in range(2):
-                for tile in groups[g]:
-                    lanes = slice(tile * LANES, (tile + 1) * LANES)
-                    value = local[comp, 7 * end, :, lanes] + x_in[end, comp, :, lanes]
-                    x_in[end, comp, :, lanes] = value
-                    row = edge_row(comp, end, tile)
-                    edge_out[0, row : row + 1, :] = value[7:8]
-                    edge_out[1, row : row + 1, :] = value[0:1]
+            take_x(pl.ds(c * CHUNK, CHUNK), x_recv.at[c])
+
+    def send_leaf(h):
+        for tile in line_tiles[h * LINES : (h + 1) * LINES]:
+            lanes = slice(tile * LANES, (tile + 1) * LANES)
+            for comp in range(comps):
+                row = line_row(comp, tile)
+                leaf = local[comp, 7 * lower, :, lanes]
+                leaf_out[0, row : row + 1, :] = leaf[7:8]
+                leaf_out[1, row : row + 1, :] = leaf[0:1]
+                own = local[comp, 7 * upper, :, lanes]
+                hub_own[0, row : row + 1, :] = own[0:1]
+                hub_own[1, row : row + 1, :] = own[7:8]
         for side in range(2):
-            when_do(target("gy", side), lambda: edge_copy(side, g).start())
-
-    def send_mid(g):
+            when_do(target("gy", side), lambda: leaf_copy(side, h).start())
+
+    def send_hub(h):
+        span = line_span(h)
+        take_both("gy", lambda sides: hub_in.at[sides, span], leaf_recv.at[h])
         for side in range(2):
-            when_do(target("gy", side), lambda: mid_copy(side, g).start())
+            hub_out[side, span] = hub_own[side, span] + hub_in[side, span]
+            there = jnp.logical_and(paired, source("gy", side))
+            when_do(there, lambda: hub_copy(side, h).start())
+
+    def send_sum(h):
+        span = line_span(h)
+        take_both("gy", lambda sides: hub_x.at[sides, span], hub_recv.at[h], paired)
+        for side in range(2):
+            line_sum[upper, side, span] = hub_out[side, span] + hub_x[side, span]
+            when_do(source("gy", side), lambda: sum_copy(side, h).start())
+
+    def wait_sum(h):
+        take_both("gy", lambda sides: line_sum.at[lower, sides, line_span(h)], sum_recv.at[h])
+
+    def send_mid(g, near):
+        for side in range(2):
+            there = jnp.logical_and(target("gy", side), way(side, near))
+            when_do(there, lambda: mid_copy(side, g).start())
 
     def wait_mid(g):
-        take_both("gy", mid_in, (pl.ds(*mid_place[g]),), mid_recv.at[g])
-
-    def wait_edge(g):
-        take_both("gy", edge_in, (pl.ds(*edge_place[g]),), edge_recv.at[g])
+        take_both("gy", lambda sides: mid_in.at[sides, pl.ds(*mid_place[g])], mid_recv.at[g])
 
     def xy_sum(comp, n, tile):
         lanes = slice(tile * LANES, (tile + 1) * LANES)
+        where = lax.broadcasted_iota(jnp.int32, (8, LANES), 0)
         if n in (0, 7):
-            value = x_in[n // 7, comp, :, lanes]
-            row = edge_row(comp, n // 7, tile)
-            sides = [edge_in[side, row : row + 1, :] for side in range(2)]
-        else:
-            value = local[comp, n, :, lanes]
-            row = mid_row(comp, n, tile)
-            sides = [mid_in[side, row : row + 1, :] for side in range(2)]
-        where = lax.broadcasted_iota(jnp.int32, value.shape, 0)
+            value = local[comp, n, :, lanes] + x_in[n // 7, comp, :, lanes]
+            row = line_row(comp, tile)
+            first, last = [line_sum[n // 7, side, row : row + 1, :] for side in range(2)]
+            value = jnp.where(where == first_line, first, value)
+            return jnp.where(where == last_line, last, value)
+        value = local[comp, n, :, lanes]
+        row = mid_row(comp, n, tile)
+        sides = [mid_in[side, row : row + 1, :] for side in range(2)]
         value = value + jnp.where(where == 0, sides[0], 0.0)
         return value + jnp.where(where == 7, sides[1], 0.0)
 
+    first_line = jnp.where(below["gy"], 0, 8)
+    last_line = jnp.where(above["gy"], 7, 8)
+
+    def outer(side):
+        return (0, 0) if side else (tiles - 1, LANES - 1)
+
     def send_z():
         for side in range(2):
-            tile, column = (tiles - 1, LANES - 1) if side == 0 else (0, 0)
+            tile, column = outer(side)
+            lanes = slice(tile * LANES, (tile + 1) * LANES)
             packed = jnp.zeros((8, LANES), jnp.float32)
             for comp in range(comps):
                 for n in range(8):
-                    value = xy_sum(comp, n, tile)[:, column : column + 1]
+                    value = local[comp, n, :, lanes][:, column : column + 1]
                     packed = jnp.where(lane == comp * 8 + n, value, packed)
             z_out[side] = packed
             when_do(target("gz", side), lambda: z_copy(side).start())
 
-    def z_column(side, comp, n):
-        at = comp * 8 + n
-        return jnp.broadcast_to(z_in[side, :, at : at + 1], (8, LANES))
+    def add_z():
+        take_both("gz", lambda sides: z_in.at[sides], z_recv)
+        for side in range(2):
+            tile, column = outer(1 - side)
+            lanes = slice(tile * LANES, (tile + 1) * LANES)
+            arrived_z = z_in[side]
+            for comp in range(comps):
+                for n in range(8):
+                    at = comp * 8 + n
+                    extra = jnp.where(lane == column, arrived_z[:, at : at + 1], 0.0)
+                    value = local[comp, n, :, lanes] + extra
+                    local[comp, n, :, lanes] = value
+                    if 0 < n < 7:
+                        put_mid(comp, n, tile, value)
 
     def finish(which, first, last):
         for comp in range(comps):
             for n in which:
                 parts = []
                 for tile in range(first - 1, last + 1):
-                    if tile < 0:
-                        parts.append(z_column(0, comp, n))
-                    elif tile == tiles:
-                        parts.append(z_column(1, comp, n))
+                    if 0 <= tile < tiles:
+                        parts.append(xy_sum(comp, n, tile))
                     else:
-                        parts.append(xy_sum(comp, n, tile))
+                        parts.append(jnp.zeros((8, LANES), jnp.float32))
                 value = jnp.concatenate(parts, axis=1)
                 width = value.shape[1]
                 before = pltpu.roll(value, 1, 1)[:, LANES:-LANES]
@@ -408,17 +546,14 @@
                 out[comp, n, :, first * LANES : last * LANES] = value[:, LANES:-LANES] + extra
 
     middle, ends = range(1, 7), (0, 7)
-    def wait_z():
-        take_both("gz", z_in, (), z_recv)
-
     finished = {middle: set(), ends: set()}
     arrived = {middle: set(), ends: set()}
 
-    def finish_ready(which, with_z):
+    def finish_ready(which):
         have = arrived[which]
 
         def near(tile):
-            return tile in have if 0 <= tile < tiles else with_z
+            return tile in have or not 0 <= tile < tiles
 
         ready = [
             tile
@@ -432,52 +567,68 @@
             finished[which].update(range(first, last + 1))
             finish(which, first, last + 1)
 
-    greeted = sum(side[name].astype(jnp.int32) for name in names for side in (below, above))
     const_copies[2].wait()
     for at, c in enumerate(order):
-        if at < 3:
+        if at < 4:
             in_copies[at].wait()
         compute(c * CHUNK, CHUNK)
         if at == 0:
             pl.semaphore_wait(barrier, greeted)
-        for side in range(2):
-            when_do(target("gx", side), lambda: x_copy(side, c).start())
+        if at == 3:
+            send_z()
+        if at == 5:
+            send_leaf(0)
+        if 0 < c < count - 2:
+            send_x(c)
         if at == 1:
-            send_mid(0)
-        if at == 5:
-            corners(0)
-        if at == 6:
-            send_mid(1)
-    send_mid(2)
-    send_mid(3)
-
-    def take(which, g, wait, with_z):
-        wait(g)
-        arrived[which].update(groups[g])
-        finish_ready(which, with_z)
-
-    corners(1)
-    wait_mid(0)
-    wait_edge(0)
-    send_z()
-    arrived[middle].update(groups[0])
-    arrived[ends].update(groups[0])
-    corners(2)
-    corners(3)
-    take(middle, 1, wait_mid, False)
-    take(middle, 2, wait_mid, False)
-    wait_z()
-    take(middle, 3, wait_mid, True)
-    for g in range(1, 4):
-        take(ends, g, wait_edge, True)
-
-    for name, ref, semaphore in (
-        ("gx", x_in, x_send),
-        ("gy", mid_in, mid_send),
-        ("gy", edge_in, edge_send),
-        ("gz", z_in, z_send),
+            send_mid(0, True)
+    add_z()
+    send_leaf(1)
+    last = (count - 2, 0, count - 1)
+    for c in last:
+        send_x(c, True)
+
+    def take_mid(g):
+        wait_mid(g)
+        arrived[middle].update(groups[g])
+        finish_ready(middle)
+
+    def take_ends(h):
+        wait_sum(h)
+        now = line_tiles[h * LINES : (h + 1) * LINES]
+        for tile in now:
+            wait_x(tile)
+        arrived[ends].update(now)
+        finish_ready(ends)
+
+    for g in (1, 2, 3):
+        send_mid(g, True)
+    send_hub(0)
+    send_hub(1)
+    for c in last:
+        send_x(c, False)
+    send_mid(0, False)
+    send_mid(1, False)
+    send_sum(0)
+    send_mid(2, False)
+    send_sum(1)
+    send_mid(3, False)
+    take_mid(0)
+    take_ends(0)
+    take_mid(1)
+    take_mid(2)
+    take_ends(1)
+    take_mid(3)
+
+    take_x(every, x_send)
+    for piece, semaphore, also in (
+        (lambda sides: mid_in.at[sides], mid_send, None),
+        (lambda sides: hub_in.at[sides], leaf_send, None),
+        (lambda sides: hub_in.at[sides], sum_send, None),
+        (lambda sides: hub_x.at[sides], hub_send, paired),
     ):
-        take_both(name, ref, (), semaphore)
+        take_both("gy", piece, semaphore, also)
+    take_both("gz", lambda sides: z_in.at[sides], z_send)
 
 
 def local_part(sizes, nodal_scalar_values, geometry):
@@ -485,7 +636,8 @@
     count = total // CHUNK
     _, groups = plan(total)
     mid_rows = offsets(groups, comps * 6)[1]
-    edge_rows = offsets(groups, comps * 2)[1]
+    line_rows = total // LANES * comps
+    line_groups = total // (LANES * LINES)
     matrices, scales = tables()
     f32 = jnp.float32
     dma = pltpu.SemaphoreType.DMA
@@ -504,18 +656,26 @@
             pltpu.VMEM((2, comps, 8, total), f32),
             pltpu.VMEM((2, mid_rows, LANES), f32),
             pltpu.VMEM((2, mid_rows, LANES), f32),
-            pltpu.VMEM((2, edge_rows, LANES), f32),
-            pltpu.VMEM((2, edge_rows, LANES), f32),
+            pltpu.VMEM((2, line_rows, LANES), f32),
+            pltpu.VMEM((2, line_rows, LANES), f32),
+            pltpu.VMEM((2, line_rows, LANES), f32),
+            pltpu.VMEM((2, line_rows, LANES), f32),
+            pltpu.VMEM((2, line_rows, LANES), f32),
+            pltpu.VMEM((2, 2, line_rows, LANES), f32),
             pltpu.VMEM((2, 8, LANES), f32),
             pltpu.VMEM((2, 8, LANES), f32),
-            dma((3,)),
+            dma((4,)),
             dma((3,)),
             dma,
             dma((count,)),
             dma,
             dma((len(groups),)),
             dma,
-            dma((len(groups),)),
+            dma((line_groups,)),
+            dma,
+            dma((line_groups,)),
+            dma,
+            dma((line_groups,)),
             dma,
             dma,
         ],

time: 26.8 us -> 25.5 us (0.951)
  the two profiles are of different devices: /device:TPU:238 before, /device:TPU:252 now
where the time goes in v4:
time: 25.5 us; the launch traced here: 25.3 us
  Pallas kernels  24.2 us (95%)
  local copies, waits for them, and re-layouts  1.15 us (5%)
    pallas_call x1, Pallas kernels, local_part(): pl.pallas_call(functools.partial(kernel, sizes), out_shape=pltpu.VMEM(nod...  24.2 us
    unnamed x1, local copies, waits for them, and re-layouts  1.15 us

profile of v4, /device:TPU:252, one launch (start us, length us, event | category | flops | bytes accessed | tf_op | source)
XLA Modules:
  0.0 25.3 jit_solution(816771866921379623)
XLA Ops:
  0.0 24.2 %poisson.1 = f32[3,8,8,2048]{3,2,1,0:T(8,128)S(1)} custom-call(f32[3,8,8,2048]{3,2,1,0:T(8,128)} %u_hbm.1, f32[6,1,1,256]{3,2,1,0:T(1,128)} %geo_hbm.1, bf16[512,256]{1,0:T(8,128)(2,1)} %constant.4.clone.mat_hbm, f32[72,128]{1,0:T(8,128)} %constant.5.clone.scale_hbm), custom_call_target="tpu_custom_call" | custom-call | tf_op jit(solution)/shard_map/poisson/pallas_call | solution.py:645
  24.2 1.1 %copy.6 = f32[3,8,8,2048]{3,2,1,0:T(8,128)} copy(f32[3,8,8,2048]{3,2,1,0:T(8,128)S(1)} %poisson.1) | data formatting | bytes 3145728

commit v5 on v4

--- a/solution.py
+++ b/solution.py
@@ -205,14 +205,6 @@
                 )
 
     greeted = sum(side[name].astype(jnp.int32) for name in names for side in (below, above))
-    for side in range(2):
-        there = jnp.logical_and(paired, source("gy", side))
-        greeted = greeted + there.astype(jnp.int32)
-
-        @pl.when(there)
-        def _(side=side):
-            pl.semaphore_signal(barrier, inc=1, device_id=across(side), device_id_type=MESH)
-
     def in_copy(at, first, last):
         span = pl.ds(first * CHUNK, (last - first) * CHUNK)
         return pltpu.make_async_copy(
@@ -235,9 +227,6 @@
     for copy in const_copies:
         copy.start()
 
-    for copy in in_copies[1:]:
-        copy.start()
-
     for side in range(2):
 
         @pl.when(jnp.logical_not(source("gx", side)))
@@ -265,7 +254,7 @@
             local.at[:, 7 if side == 0 else 0, rows, span],
             x_in.at[side, :, rows, span],
             x_send,
-            x_recv.at[c],
+            x_recv.at[line_at[c * PER] // LINES],
             device_id=neighbour("gx", side),
             device_id_type=MESH,
         )
@@ -361,6 +350,8 @@
 
     for copy in const_copies[:2]:
         copy.wait()
+    for copy in in_copies[1:]:
+        copy.start()
     rows = jnp.concatenate(
         [geo[k, 0] for k in range(6)] + [jnp.zeros((2, geo.shape[-1]), jnp.float32)], axis=0
     )
@@ -432,13 +423,8 @@
         mid_out[0, row : row + 1, :] = value[7:8]
         mid_out[1, row : row + 1, :] = value[0:1]
 
-    x_here = set()
-
-    def wait_x(tile):
-        c = tile // PER
-        if c not in x_here:
-            x_here.add(c)
-            take_x(pl.ds(c * CHUNK, CHUNK), x_recv.at[c])
+    def wait_x(h):
+        take_x(pl.ds(0, LINES * LANES), x_recv.at[h])
 
     def send_leaf(h):
         for tile in line_tiles[h * LINES : (h + 1) * LINES]:
@@ -572,13 +558,14 @@
         if at < 4:
             in_copies[at].wait()
         compute(c * CHUNK, CHUNK)
-        if at == 0:
+        if at == 1:
             pl.semaphore_wait(barrier, greeted)
+            send_x(order[0])
         if at == 3:
             send_z()
         if at == 5:
             send_leaf(0)
-        if 0 < c < count - 2:
+        if at and 0 < c < count - 2:
             send_x(c)
         if at == 1:
             send_mid(0, True)
@@ -596,8 +583,7 @@
     def take_ends(h):
         wait_sum(h)
         now = line_tiles[h * LINES : (h + 1) * LINES]
-        for tile in now:
-            wait_x(tile)
+        wait_x(h)
         arrived[ends].update(now)
         finish_ready(ends)
 
@@ -667,7 +653,7 @@
             dma((4,)),
             dma((3,)),
             dma,
-            dma((count,)),
+            dma((line_groups,)),
             dma,
             dma((len(groups),)),
             dma,

time: 25.5 us -> 25.4 us (level)
  the two profiles are of different devices: /device:TPU:252 before, /device:TPU:254 now
where the time goes in v5:
time: 25.4 us; the launch traced here: 25.3 us
  Pallas kernels  24.1 us (95%)
  local copies, waits for them, and re-layouts  1.15 us (5%)
    pallas_call x1, Pallas kernels, local_part(): pl.pallas_call(functools.partial(kernel, sizes), out_shape=pltpu.VMEM(nod...  24.1 us
    unnamed x1, local copies, waits for them, and re-layouts  1.15 us

profile of v5, /device:TPU:254, one launch (start us, length us, event | category | flops | bytes accessed | tf_op | source)
XLA Modules:
  0.0 25.3 jit_solution(17081045782528912494)
XLA Ops:
  0.0 24.1 %poisson.1 = f32[3,8,8,2048]{3,2,1,0:T(8,128)S(1)} custom-call(f32[3,8,8,2048]{3,2,1,0:T(8,128)} %u_hbm.1, f32[6,1,1,256]{3,2,1,0:T(1,128)} %geo_hbm.1, bf16[512,256]{1,0:T(8,128)(2,1)} %constant.4.clone.mat_hbm, f32[72,128]{1,0:T(8,128)} %constant.5.clone.scale_hbm), custom_call_target="tpu_custom_call" | custom-call | tf_op jit(solution)/shard_map/poisson/pallas_call | solution.py:631
  24.1 1.1 %copy.6 = f32[3,8,8,2048]{3,2,1,0:T(8,128)} copy(f32[3,8,8,2048]{3,2,1,0:T(8,128)S(1)} %poisson.1) | data formatting | bytes 3145728

commit v6 on v5

--- a/solution.py
+++ b/solution.py
@@ -558,14 +558,13 @@
         if at < 4:
             in_copies[at].wait()
         compute(c * CHUNK, CHUNK)
-        if at == 1:
+        if at == 0:
             pl.semaphore_wait(barrier, greeted)
-            send_x(order[0])
         if at == 3:
             send_z()
         if at == 5:
             send_leaf(0)
-        if at and 0 < c < count - 2:
+        if 0 < c < count - 2:
             send_x(c)
         if at == 1:
             send_mid(0, True)
@@ -591,11 +590,11 @@
         send_mid(g, True)
     send_hub(0)
     send_hub(1)
-    for c in last:
-        send_x(c, False)
     send_mid(0, False)
     send_mid(1, False)
     send_sum(0)
+    for c in last:
+        send_x(c, False)
     send_mid(2, False)
     send_sum(1)
     send_mid(3, False)

time: 25.4 us -> 25.3 us (level)
  the two profiles are of different devices: /device:TPU:254 before, /device:TPU:221 now
where the time goes in v6:
time: 25.3 us; the launch traced here: 25.1 us
  Pallas kernels  24 us (95%)
  local copies, waits for them, and re-layouts  1.15 us (5%)
    pallas_call x1, Pallas kernels, local_part(): pl.pallas_call(functools.partial(kernel, sizes), out_shape=pltpu.VMEM(nod...  24 us
    unnamed x1, local copies, waits for them, and re-layouts  1.15 us

profile of v6, /device:TPU:221, one launch (start us, length us, event | category | flops | bytes accessed | tf_op | source)
XLA Modules:
  0.0 25.1 jit_solution(17760086776022850036)
XLA Ops:
  0.0 24.0 %poisson.1 = f32[3,8,8,2048]{3,2,1,0:T(8,128)S(1)} custom-call(f32[3,8,8,2048]{3,2,1,0:T(8,128)} %u_hbm.1, f32[6,1,1,256]{3,2,1,0:T(1,128)} %geo_hbm.1, bf16[512,256]{1,0:T(8,128)(2,1)} %constant.4.clone.mat_hbm, f32[72,128]{1,0:T(8,128)} %constant.5.clone.scale_hbm), custom_call_target="tpu_custom_call" | custom-call | tf_op jit(solution)/shard_map/poisson/pallas_call | solution.py:630
  24.0 1.1 %copy.6 = f32[3,8,8,2048]{3,2,1,0:T(8,128)} copy(f32[3,8,8,2048]{3,2,1,0:T(8,128)S(1)} %poisson.1) | data formatting | bytes 3145728

commit v7 on v6

--- a/solution.py
+++ b/solution.py
@@ -152,11 +152,9 @@
     x_recv,
     mid_send,
     mid_recv,
-    leaf_send,
     leaf_recv,
     hub_send,
     hub_recv,
-    sum_send,
     sum_recv,
     z_send,
     z_recv,
@@ -277,7 +275,7 @@
         return pltpu.make_async_remote_copy(
             leaf_out.at[side, line_span(h)],
             hub_in.at[side, line_span(h)],
-            leaf_send,
+            mid_send,
             leaf_recv.at[h],
             device_id=neighbour("gy", side),
             device_id_type=MESH,
@@ -297,7 +295,7 @@
         return pltpu.make_async_remote_copy(
             line_sum.at[upper, side, line_span(h)],
             line_sum.at[upper, 1 - side, line_span(h)],
-            sum_send,
+            mid_send,
             sum_recv.at[h],
             device_id={"gy": place["gy"] + (1 if side else -1)},
             device_id_type=MESH,
@@ -599,17 +597,15 @@
     send_sum(1)
     send_mid(3, False)
     take_mid(0)
+    take_mid(1)
     take_ends(0)
-    take_mid(1)
     take_mid(2)
     take_ends(1)
     take_mid(3)
 
     take_x(every, x_send)
     for piece, semaphore, also in (
-        (lambda sides: mid_in.at[sides], mid_send, None),
-        (lambda sides: hub_in.at[sides], leaf_send, None),
-        (lambda sides: hub_in.at[sides], sum_send, None),
+        (lambda sides: x_in.at[sides], mid_send, None),
         (lambda sides: hub_x.at[sides], hub_send, paired),
     ):
         take_both("gy", piece, semaphore, also)
@@ -655,11 +651,9 @@
             dma((line_groups,)),
             dma,
             dma((len(groups),)),
-            dma,
             dma((line_groups,)),
             dma,
             dma((line_groups,)),
-            dma,
             dma((line_groups,)),
             dma,
             dma,

time: 25.3 us -> 25.2 us (level)
  no operation moved by 1% of the time
where the time goes in v7:
time: 25.2 us; the launch traced here: 25.1 us
  Pallas kernels  23.9 us (95%)
  local copies, waits for them, and re-layouts  1.15 us (5%)
    pallas_call x1, Pallas kernels, local_part(): pl.pallas_call(functools.partial(kernel, sizes), out_shape=pltpu.VMEM(nod...  23.9 us
    unnamed x1, local copies, waits for them, and re-layouts  1.15 us

profile of v7, /device:TPU:221, one launch (start us, length us, event | category | flops | bytes accessed | tf_op | source)
XLA Modules:
  0.0 25.1 jit_solution(2965021160685207050)
XLA Ops:
  0.0 23.9 %poisson.1 = f32[3,8,8,2048]{3,2,1,0:T(8,128)S(1)} custom-call(f32[3,8,8,2048]{3,2,1,0:T(8,128)} %u_hbm.1, f32[6,1,1,256]{3,2,1,0:T(1,128)} %geo_hbm.1, bf16[512,256]{1,0:T(8,128)(2,1)} %constant.4.clone.mat_hbm, f32[72,128]{1,0:T(8,128)} %constant.5.clone.scale_hbm), custom_call_target="tpu_custom_call" | custom-call | tf_op jit(solution)/shard_map/poisson/pallas_call | solution.py:626
  23.9 1.1 %copy.6 = f32[3,8,8,2048]{3,2,1,0:T(8,128)} copy(f32[3,8,8,2048]{3,2,1,0:T(8,128)S(1)} %poisson.1) | data formatting | bytes 3145728
